TPU v7x, 256 devices: a 8x8x2 block of a 8x8x16 slice. The times are simulated.
256 devices in a mesh: slab: 2 (over z), row: 128 (over y, x, core).
Axes of the slice: x: 8, y: 8, z: 2, core: 2. Of those that a mesh axis runs over, the one named last changes fastest.
The devices are a block of a 8x8x16 slice.
Arguments:
- raw_echo: float32 [2, 8192, 16384], P(None, 'slab', 'row'), parts along dimension 1, may hold values from -6 to 6
- centroid: int32 [64], P('slab'), parts along dimension 0, may hold values from 0 to 16383
- shifts: int32 [64], P('slab'), parts along dimension 0, may hold values from 0 to 12, as said below
- chirp_rate: float32 [8192], P(('slab', 'row')), parts along dimension 0, may hold values from 50 to 400
Outputs:
- focused_image: float32 [2, 8192, 16384], P(None, ('slab', 'row')), parts along dimension 1
There are 2 independent parts, one for each index of `slab`. A program takes and returns all parts, laid end to end along the dimension named above; each array names one. Nothing has to cross between parts.
Inputs may be any that keep to these rules, and one draw needn't show every extreme that they name: `shifts`: range migration of each block in range bins; some block reaches 12 in every draw.
All inputs are finite; a program needn't handle non-finite values.
Results may differ from a plain program's by a relative error of at most 0.0003.
Values sent between devices are 32-bit elements; how exact they have to be, the bound alone decides.
No kernel may reach another device: no remote copies, remote signals or barrier semaphores. Data moves between devices by JAX's collectives and lax.ppermute only.
A program may use at most 128 MiB of HBM per device.

v0:
```python
import math

import jax
import jax.numpy as jnp
from jax import lax
from jax.sharding import PartitionSpec as P

FACTOR = 128
PULSES = 16384
BLOCK = 128
MAXSHIFT = 12
TAPS = 4


def from_behind(shard, axis, by):
    devices = lax.axis_size(axis)
    pairs = [(i, i + by) for i in range(devices) if 0 <= i + by < devices]
    return lax.ppermute(shard, axis, pairs)


def transform_table(length, modulus, inverse):
    indices = jnp.arange(length, dtype=jnp.int32)
    product = indices[:, None] * indices[None, :] % modulus
    angles = 2.0 * math.pi / modulus * product.astype(jnp.float32)
    if inverse:
        return (jnp.cos(angles), jnp.sin(angles))
    return (jnp.cos(angles), -jnp.sin(angles))


def contract(table_real, table_imag, real_part, imag_part, pattern):

    def product(matrix, operand):
        return jnp.einsum(pattern, matrix, operand, precision=lax.Precision.HIGHEST)

    return (
        product(table_real, real_part) - product(table_imag, imag_part),
        product(table_real, imag_part) + product(table_imag, real_part),
    )


def transform(real_part, imag_part, inverse):
    leading = real_part.shape[:-1]
    real_part = real_part.reshape(leading + (FACTOR, FACTOR))
    imag_part = imag_part.reshape(leading + (FACTOR, FACTOR))
    base_real, base_imag = transform_table(FACTOR, FACTOR, inverse)
    twist_real, twist_imag = transform_table(FACTOR, FACTOR * FACTOR, inverse)
    first_real, first_imag = contract(base_real, base_imag, real_part, imag_part, "ab,...bc->...ac")
    turned_real = first_real * twist_real - first_imag * twist_imag
    turned_imag = first_real * twist_imag + first_imag * twist_real
    second_real, second_imag = contract(
        base_real, base_imag, turned_real, turned_imag, "ab,...cb->...ac"
    )
    return (
        second_real.reshape(leading + (FACTOR * FACTOR,)),
        second_imag.reshape(leading + (FACTOR * FACTOR,)),
    )


def kernel(offsets):
    inside = jnp.abs(offsets) < TAPS
    tapering = jnp.cos(math.pi * offsets / (2.0 * TAPS))
    return jnp.where(inside, jnp.sinc(offsets) * tapering * tapering, 0.0)


def spectral(pieces):
    result = transform(pieces[0, 0], pieces[1, 0], False)
    return jnp.stack(result)


def per_device(raw_echo, centroid, shifts, chirp_rate):
    devices = lax.axis_size("row")
    total_rows = raw_echo.shape[1]
    pulse_share = raw_echo.shape[2]
    own_rows = total_rows // devices
    lower_rim = TAPS - 1
    upper_rim = MAXSHIFT + TAPS - 1
    blocks = raw_echo.reshape(2, devices, own_rows, pulse_share)
    spectrum = spectral(lax.all_to_all(blocks, "row", split_axis=1, concat_axis=3, tiled=True))
    above_rows = from_behind(spectrum[:, :upper_rim], "row", -1)
    below_rows = from_behind(spectrum[:, own_rows - lower_rim :], "row", 1)
    extended = jnp.concatenate([below_rows, spectrum, above_rows], axis=1)
    device_index = lax.axis_index("row")
    local_blocks = max(own_rows // BLOCK, 1)
    block_rows = own_rows // local_blocks
    first_block = device_index * own_rows // BLOCK
    block_ids = first_block + jnp.arange(local_blocks, dtype=jnp.int32)
    chosen = block_ids[:, None] == jnp.arange(centroid.shape[0], dtype=jnp.int32)[None, :]
    centers = jnp.sum(jnp.where(chosen, centroid[None, :], 0), axis=1)
    distances = jnp.sum(jnp.where(chosen, shifts[None, :], 0), axis=1)
    doppler_bins = jnp.arange(PULSES, dtype=jnp.int32)
    wrapped = (doppler_bins[None, :] - centers[:, None] + PULSES // 2) % PULSES - PULSES // 2
    relative = wrapped.astype(jnp.float32) / PULSES
    migration = distances[:, None].astype(jnp.float32) * 4.0 * relative * relative

    def grouped(rows):
        return rows.reshape(local_blocks, block_rows, PULSES)

    weight = kernel(-lower_rim - migration)[:, None, :]
    real_sum = weight * grouped(extended[0, 0:own_rows])
    imag_sum = weight * grouped(extended[1, 0:own_rows])
    for offset in range(1 - lower_rim, upper_rim + 1):
        weight = kernel(offset - migration)[:, None, :]
        start_row = offset + lower_rim
        real_sum = real_sum + weight * grouped(extended[0, start_row : start_row + own_rows])
        imag_sum = imag_sum + weight * grouped(extended[1, start_row : start_row + own_rows])
    window = (0.54 + 0.46 * jnp.cos(2.0 * math.pi * relative))[:, None, :]
    rates = chirp_rate.reshape(local_blocks, block_rows)
    phase_angle = math.pi * rates[:, :, None] * (relative * relative)[:, None, :]
    cosine = jnp.cos(phase_angle)
    sine_part = jnp.sin(phase_angle)
    focus_real = (window * (real_sum * cosine + imag_sum * sine_part)).reshape(own_rows, PULSES)
    focus_imag = (window * (imag_sum * cosine - real_sum * sine_part)).reshape(own_rows, PULSES)
    image_real, image_imag = transform(focus_real, focus_imag, True)
    return jnp.stack([image_real, image_imag]) / PULSES


def solution(mesh):
    return jax.shard_map(
        per_device,
        mesh=mesh,
        in_specs=(P(None, "slab", "row"), P("slab"), P("slab"), P(("slab", "row"))),
        out_specs=P(None, ("slab", "row"), None),
        check_vma=False,
    )
```

profile of v0, /device:TPU:519, one launch (start us, length us, event | category | flops | bytes accessed | tf_op | source)
XLA Modules:
  0.0 291.0 jit_solution(8760837651498275698)
XLA Ops:
  0.0 4.8 %copy.26 = f32[2,128,32,128]{3,2,0,1:T(8,128)} copy(f32[2,128,32,128]{3,2,1,0:T(8,128)} %bitcast.136) | data formatting | bytes 8388608 | tf_op jit(solution)/shard_map/reshape | solution.py:77
  4.9 27.9 %all-to-all-start = ((f32[2,128,32,128]{3,2,0,1:T(8,128)}), f32[2,128,32,128]{3,2,0,1:T(8,128)}, u32[]{:S(2)}, u32[]{:S(2)}) async-start(f32[2,128,32,128]{3,2,0,1:T(8,128)} %copy.26), calls=%async_computation | async-start | bytes 8388608 | tf_op jit(solution)/shard_map/all_to_all | solution.py:78
  34.7 5.6 %compare_select_fusion.75 = (f32[1,16384]{1,0:T(1,128)S(1)}, f32[1,16384]{1,0:T(1,128)S(1)}) fusion(f32[]{:T(128)S(6)} %mul.1421, s32[]{:T(128)} %fusion.278), kind=kLoop, calls=%fused_computation.297 | loop fusion | flops 1572864 | bytes 131080 | tf_op jit(solution)/shard_map/jit(_where)/select_n | solution.py:62
  40.3 5.6 %compare_select_fusion.73 = (f32[1,16384]{1,0:T(1,128)S(1)}, f32[1,16384]{1,0:T(1,128)S(1)}) fusion(f32[]{:T(128)S(6)} %mul.1421, s32[]{:T(128)} %fusion.278), kind=kLoop, calls=%fused_computation.295 | loop fusion | flops 1572864 | bytes 131080 | tf_op jit(solution)/shard_map/jit(_where)/select_n | solution.py:62
  46.0 5.6 %compare_select_fusion.71 = (f32[1,16384]{1,0:T(1,128)S(1)}, f32[1,16384]{1,0:T(1,128)S(1)}) fusion(f32[]{:T(128)S(6)} %mul.1421, s32[]{:T(128)} %fusion.278), kind=kLoop, calls=%fused_computation.293 | loop fusion | flops 1572864 | bytes 131080 | tf_op jit(solution)/shard_map/jit(_where)/select_n | solution.py:62
  51.6 5.6 %compare_select_fusion.69 = (f32[1,16384]{1,0:T(1,128)S(1)}, f32[1,16384]{1,0:T(1,128)S(1)}) fusion(f32[]{:T(128)S(6)} %mul.1421, s32[]{:T(128)} %fusion.278), kind=kLoop, calls=%fused_computation.291 | loop fusion | flops 1572864 | bytes 131080 | tf_op jit(solution)/shard_map/jit(_where)/select_n | solution.py:62
  58.8 5.6 %compare_select_fusion.67 = (f32[1,16384]{1,0:T(1,128)S(1)}, f32[1,16384]{1,0:T(1,128)S(1)}) fusion(f32[]{:T(128)S(6)} %mul.1421, s32[]{:T(128)} %fusion.278), kind=kLoop, calls=%fused_computation.289 | loop fusion | flops 1572864 | bytes 131080 | tf_op jit(solution)/shard_map/jit(_where)/select_n | solution.py:62
  64.5 5.6 %compare_select_fusion.65 = (f32[1,16384]{1,0:T(1,128)S(1)}, f32[1,16384]{1,0:T(1,128)S(1)}) fusion(f32[]{:T(128)S(6)} %mul.1421, s32[]{:T(128)} %fusion.278), kind=kLoop, calls=%fused_computation.287 | loop fusion | flops 1572864 | bytes 131080 | tf_op jit(solution)/shard_map/jit(_where)/select_n | solution.py:62
  70.1 5.6 %compare_select_fusion.63 = (f32[1,16384]{1,0:T(1,128)S(1)}, f32[1,16384]{1,0:T(1,128)S(1)}) fusion(f32[]{:T(128)S(6)} %mul.1421, s32[]{:T(128)} %fusion.278), kind=kLoop, calls=%fused_computation.285 | loop fusion | flops 1572864 | bytes 131080 | tf_op jit(solution)/shard_map/jit(_where)/select_n | solution.py:62
  75.8 5.6 %compare_select_fusion.61 = (f32[1,16384]{1,0:T(1,128)S(1)}, f32[1,16384]{1,0:T(1,128)S(1)}) fusion(f32[]{:T(128)S(6)} %mul.1421, s32[]{:T(128)} %fusion.278), kind=kLoop, calls=%fused_computation.283 | loop fusion | flops 1572864 | bytes 131080 | tf_op jit(solution)/shard_map/jit(_where)/select_n | solution.py:62
  81.4 6.6 %compare_select_fusion.59 = (f32[1,16384]{1,0:T(1,128)S(1)}, f32[1,16384]{1,0:T(1,128)}) fusion(f32[]{:T(128)S(6)} %mul.1421, s32[]{:T(128)} %fusion.278), kind=kLoop, calls=%fused_computation.281 | loop fusion | flops 1572864 | bytes 131080 | tf_op jit(solution)/shard_map/jit(_where)/select_n | solution.py:62
  88.0 42.8 %all-to-all-done = f32[2,128,32,128]{3,2,0,1:T(8,128)} async-done(((f32[2,128,32,128]{3,2,0,1:T(8,128)}), f32[2,128,32,128]{3,2,0,1:T(8,128)}, u32[]{:S(2)}, u32[]{:S(2)}) %all-to-all-start) | async-done | bytes 4194336 | tf_op jit(solution)/shard_map/all_to_all | solution.py:78
  130.8 4.6 %copy.55 = f32[2,128,32,128]{3,1,2,0:T(8,128)S(1)} copy(f32[2,128,32,128]{3,2,0,1:T(8,128)} %all-to-all-done) | data formatting | bytes 8388608 | tf_op jit(solution)/shard_map/all_to_all | solution.py:78
  135.4 2.1 fusion.127
  137.6 2.1 fusion.126
  139.7 2.3 fusion.130
  142.0 2.2 fusion.131
  144.2 2.4 fusion.118
  146.6 3.4 %fusion.120 = f32[32,128,128]{2,1,0:T(8,128)} fusion(f32[128,32,128]{2,0,1:T(8,128)S(1)} %fusion.131, f32[128,32,128]{2,0,1:T(8,128)S(1)} %fusion.130, f32[128,128]{1,0:T(8,128)S(1)} %get-tuple-element.28, f32[128,128]{1,0:T(8,128)S(1)} %get-tuple-element.27), kind=kOutput, calls=%fused_computation.200 | convolution fusion | flops 807124992 | bytes 6422528 | tf_op jit(solution)/shard_map/ab,...cb->...ac/dot_general | solution.py:33
  150.0 3.6 %add_bitcast_fusion.1 = f32[32,128,128]{1,2,0:T(8,128)} fusion(f32[32,128,128]{2,1,0:T(8,128)S(1)} %fusion.118, f32[128,32,128]{2,0,1:T(8,128)S(1)} %fusion.131, f32[128,32,128]{2,0,1:T(8,128)S(1)} %fusion.130, f32[128,128]{1,0:T(8,128)S(1)} %get-tuple-element.28, f32[128,128]{1,0:T(8,128)S(1)} %get-tuple-element.27), kind=kOutput, calls=%fused_computation.208 | convolution fusion | flops 807649280 | bytes 8519680 | tf_op jit(solution)/shard_map/ab,...cb->...ac/dot_general | solution.py:33
  153.6 2.9 %copy.29 = f32[32,128,128]{2,1,0:T(8,128)} copy(f32[32,128,128]{1,2,0:T(8,128)} %add_bitcast_fusion.1) | data formatting | bytes 4194304 | tf_op jit(solution)/shard_map/add | solution.py:37
  156.6 2.7 stack_reshape.13
  159.3 5.6 %subtract_bitcast_fusion.1 = f32[32,128,128]{1,2,0:T(8,128)} fusion(f32[32,128,128]{2,1,0:T(8,128)} %fusion.120, f32[128,32,128]{2,0,1:T(8,128)} %copy-done, f32[128,32,128]{2,0,1:T(8,128)S(1)} %fusion.130, f32[128,128]{1,0:T(8,128)S(1)} %get-tuple-element.28, f32[128,128]{1,0:T(8,128)S(1)} %get-tuple-element.27), kind=kOutput, calls=%fused_computation.209 | convolution fusion | flops 807632896 | bytes 8519680 | tf_op jit(solution)/shard_map/ab,...cb->...ac/dot_general | solution.py:33
  164.9 2.9 %copy.28 = f32[32,128,128]{2,1,0:T(8,128)} copy(f32[32,128,128]{1,2,0:T(8,128)} %subtract_bitcast_fusion.1) | data formatting | bytes 4194304 | tf_op jit(solution)/shard_map/sub | solution.py:36
  167.8 1.7 stack_reshape.12
  169.7 1.4 copy-done.2
  171.5 1.5 copy.30
  173.0 3.2 %collective-permute-start.1 = (f32[2,15,16384]{2,0,1:T(2,128)S(1)}, f32[2,15,16384]{2,0,1:T(2,128)S(1)}, u32[]{:S(2)}, u32[]{:S(2)}) collective-permute-start(f32[2,15,16384]{2,0,1:T(2,128)S(1)} %copy.30), channel_id=1, source_target_pairs={{1,0},{2,1},{3,2},{4,3},{5,4},{6,5},{7,6},{8,7},{9,8},{10,9},{11,1... | collective-permute-start | bytes 5898248 | tf_op jit(solution)/shard_map/ppermute | solution.py:18
  176.2 3.3 %compare_select_fusion.77 = f32[1,16384]{1,0:T(1,128)S(1)} fusion(f32[]{:T(128)S(6)} %mul.1421, s32[]{:T(128)} %fusion.278), kind=kLoop, calls=%fused_computation.299 | loop fusion | flops 933888 | bytes 65544 | tf_op jit(solution)/shard_map/jit(_where)/select_n | solution.py:62
  179.5 3.7 %collective-permute-start = (f32[2,3,16384]{2,1,0:T(4,128)S(1)}, f32[2,3,16384]{2,1,0:T(4,128)S(1)}, u32[]{:S(2)}, u32[]{:S(2)}) collective-permute-start(f32[2,3,16384]{2,1,0:T(4,128)S(1)} %slice.200), channel_id=1, source_target_pairs={{0,1},{1,2},{2,3},{3,4},{4,5},{5,6},{6,7},{7,8},{8,9},{9,10},{10,1... | collective-permute-start | bytes 1179656 | tf_op jit(solution)/shard_map/ppermute | solution.py:18
  183.9 16.3 %collective-permute-done.1 = f32[2,15,16384]{2,0,1:T(2,128)S(1)} collective-permute-done((f32[2,15,16384]{2,0,1:T(2,128)S(1)}, f32[2,15,16384]{2,0,1:T(2,128)S(1)}, u32[]{:S(2)}, u32[]{:S(2)}) %collective-permute-start.1) | collective-permute-done | bytes 1966112 | tf_op jit(solution)/shard_map/ppermute | solution.py:18
  200.2 2.5 copy.31
  202.7 28.3 %fusion.9 = (f32[4,8,128,128]{3,1,2,0:T(8,128)}, f32[1,32,16384]{2,1,0:T(8,128)S(1)}, f32[1,32,16384]{2,1,0:T(8,128)S(1)}) fusion(f32[16384]{0:T(1024)S(1)} %multiply_multiply_fusion.38, f32[32]{0:T(128)S(1)} %broadcast_multiply_fusion, f32[16384]{0:T(1024)S(1)} %multiply_add_fusion.22, f32[16384]{0:T(1024)S(1)} %bitcast.153, f32[16384]{0:T(1024)S(1)} %bitcast.154, ...), kind=kLoop, calls=%fused_computation.81 | loop fusion | flops 60293120 | bytes 18415744
  231.0 8.3 %fusion.6 = f32[4,8,128,128]{3,1,2,0:T(8,128)S(1)} fusion(f32[1,32,16384]{2,1,0:T(8,128)S(1)} %get-tuple-element.8, f32[1,32,16384]{2,1,0:T(8,128)S(1)} %get-tuple-element.7, f32[16384]{0:T(1024)S(1)} %multiply_multiply_fusion.38, f32[32]{0:T(128)S(1)} %broadcast_multiply_fusion, f32[16384]{0:T(1024)S(1)} %multiply_add_fusion.22), kind=kLoop, calls=%fused_computation.78 | loop fusion | flops 2621440 | bytes 6422656
  239.7 1.2 copy-done.3
  241.2 3.6 %fusion.175 = f32[32,128,128]{2,1,0:T(8,128)S(1)} fusion(f32[32,128,128]{2,1,0:T(8,128)S(1)} %bitcast.134), kind=kOutput, calls=%fused_computation.418 | convolution fusion | flops 805535744 | bytes 4194304 | tf_op jit(solution)/shard_map/ab,...bc->...ac/dot_general | solution.py:33
  244.8 3.6 %fusion.173 = f32[32,128,128]{2,1,0:T(8,128)S(1)} fusion(f32[32,128,128]{2,1,0:T(8,128)S(1)} %bitcast.132), kind=kOutput, calls=%fused_computation.416 | convolution fusion | flops 805535744 | bytes 4194304 | tf_op jit(solution)/shard_map/ab,...bc->...ac/dot_general | solution.py:33
  248.4 3.7 %convolution_subtract_fusion = f32[32,128,128]{2,1,0:T(8,128)S(1)} fusion(f32[32,128,128]{2,1,0:T(8,128)S(1)} %fusion.175, f32[32,128,128]{2,1,0:T(8,128)S(1)} %bitcast.133), kind=kOutput, calls=%fused_computation.219 | convolution fusion | flops 806060032 | bytes 6291456 | tf_op jit(solution)/shard_map/ab,...bc->...ac/dot_general | solution.py:33
  252.1 3.8 %convolution_add_fusion = f32[32,128,128]{2,1,0:T(8,128)S(1)} fusion(f32[32,128,128]{2,1,0:T(8,128)S(1)} %fusion.173, f32[32,128,128]{2,1,0:T(8,128)S(1)} %bitcast.135), kind=kOutput, calls=%fused_computation.218 | convolution fusion | flops 806060032 | bytes 6291456 | tf_op jit(solution)/shard_map/ab,...bc->...ac/dot_general | solution.py:33
  255.8 3.8 %fusion.140 = f32[32,128,128]{2,1,0:T(8,128)S(1)} fusion(f32[32,128,128]{2,1,0:T(8,128)S(1)} %convolution_add_fusion, f32[32,128,128]{2,1,0:T(8,128)S(1)} %convolution_subtract_fusion, f32[128,128]{0,1:T(8,128)S(1)} %copy.37, f32[128,128]{0,1:T(8,128)S(1)} %copy.34), kind=kOutput, calls=%fused_computation.221 | convolution fusion | flops 807108608 | bytes 6422528 | tf_op jit(solution)/shard_map/ab,...cb->...ac/dot_general | solution.py:33
  259.6 5.0 %fusion.136 = f32[32,128,128]{2,1,0:T(8,128)} fusion(f32[32,128,128]{2,1,0:T(8,128)S(1)} %convolution_add_fusion, f32[32,128,128]{2,1,0:T(8,128)S(1)} %convolution_subtract_fusion, f32[128,128]{0,1:T(8,128)S(1)} %copy.37, f32[128,128]{0,1:T(8,128)S(1)} %copy.34), kind=kOutput, calls=%fused_computation.220 | convolution fusion | flops 807108608 | bytes 6422528 | tf_op jit(solution)/shard_map/ab,...cb->...ac/dot_general | solution.py:33
  264.6 5.3 %subtract_bitcast_fusion = f32[32,128,128]{1,2,0:T(8,128)} fusion(f32[32,128,128]{2,1,0:T(8,128)S(1)} %fusion.140, f32[32,128,128]{2,1,0:T(8,128)S(1)} %convolution_add_fusion, f32[32,128,128]{2,1,0:T(8,128)S(1)} %convolution_subtract_fusion, f32[128,128]{0,1:T(8,128)S(1)} %copy.37, f32[128,128]{0,1:T(8,128)S(1)} %copy.34), kind=kOutput, calls=%fused_computation.207 | convolution fusion | flops 807632896 | bytes 8519680 | tf_op jit(solution)/shard_map/ab,...cb->...ac/dot_general | solution.py:33
  269.9 2.9 %copy.40 = f32[32,128,128]{2,1,0:T(8,128)} copy(f32[32,128,128]{1,2,0:T(8,128)} %subtract_bitcast_fusion) | data formatting | bytes 4194304 | tf_op jit(solution)/shard_map/sub | solution.py:36
  272.8 2.7 stack_reshape.14
  275.6 7.2 %add_bitcast_fusion = f32[32,128,128]{1,2,0:T(8,128)} fusion(f32[32,128,128]{2,1,0:T(8,128)} %fusion.136, f32[32,128,128]{2,1,0:T(8,128)} %copy-done.1, f32[32,128,128]{2,1,0:T(8,128)S(1)} %convolution_subtract_fusion, f32[128,128]{0,1:T(8,128)S(1)} %copy.37, f32[128,128]{0,1:T(8,128)S(1)} %copy.34), kind=kOutput, calls=%fused_computation.206 | convolution fusion | flops 807632896 | bytes 8519680 | tf_op jit(solution)/shard_map/ab,...cb->...ac/dot_general | solution.py:33
  282.7 1.9 copy.43
  284.7 1.6 stack_reshape.15
  286.2 4.5 %maximum_multiply_fusion = f32[2,32,16384]{2,1,0:T(8,128)} fusion(f32[1,32,16384]{2,1,0:T(8,128)} %stack_reshape.15, f32[1,32,16384]{2,1,0:T(8,128)} %stack_reshape.14), kind=kLoop, calls=%fused_computation.68 | loop fusion | flops 2097152 | bytes 8388608 | tf_op jit(solution)/shard_map/div | solution.py:114
  (30 shorter events, 4.8 us)
Async XLA Ops:
  4.8 27.9 %copy-start.5 = (s32[32]{0:T(128)S(1)}, s32[32]{0:T(128)}, u32[]{:S(2)}) copy-start(s32[32]{0:T(128)} %param.6) | copy-start | bytes 388
  4.8 28.5 %copy-start.6 = (s32[32]{0:T(128)S(1)}, s32[32]{0:T(128)}, u32[]{:S(2)}) copy-start(s32[32]{0:T(128)} %param.7) | copy-start | bytes 388
  4.9 125.9 %all-to-all-start = ((f32[2,128,32,128]{3,2,0,1:T(8,128)}), f32[2,128,32,128]{3,2,0,1:T(8,128)}, u32[]{:S(2)}, u32[]{:S(2)}) async-start(f32[2,128,32,128]{3,2,0,1:T(8,128)} %copy.26), calls=%async_computation | async-start | bytes 8388608 | tf_op jit(solution)/shard_map/all_to_all | solution.py:78
  144.2 5.8 %copy-start = (f32[128,32,128]{2,0,1:T(8,128)}, f32[128,32,128]{2,0,1:T(8,128)S(1)}, u32[]{:S(2)}) copy-start(f32[128,32,128]{2,0,1:T(8,128)S(1)} %fusion.131) | copy-start | bytes 6291460
  169.6 1.6 copy-start.2
  171.5 11.8 %copy-start.7 = (f32[32]{0:T(128)S(1)}, f32[32]{0:T(128)}, u32[]{:S(2)}) copy-start(f32[32]{0:T(128)} %param.8) | copy-start | bytes 388
  173.0 27.2 %collective-permute-start.1 = (f32[2,15,16384]{2,0,1:T(2,128)S(1)}, f32[2,15,16384]{2,0,1:T(2,128)S(1)}, u32[]{:S(2)}, u32[]{:S(2)}) collective-permute-start(f32[2,15,16384]{2,0,1:T(2,128)S(1)} %copy.30), channel_id=1, source_target_pairs={{1,0},{2,1},{3,2},{4,3},{5,4},{6,5},{7,6},{8,7},{9,8},{10,9},{11,1... | collective-permute-start | bytes 5898248 | tf_op jit(solution)/shard_map/ppermute | solution.py:18
  179.5 23.1 %collective-permute-start = (f32[2,3,16384]{2,1,0:T(4,128)S(1)}, f32[2,3,16384]{2,1,0:T(4,128)S(1)}, u32[]{:S(2)}, u32[]{:S(2)}) collective-permute-start(f32[2,3,16384]{2,1,0:T(4,128)S(1)} %slice.200), channel_id=1, source_target_pairs={{0,1},{1,2},{2,3},{3,4},{4,5},{5,6},{6,7},{7,8},{8,9},{9,10},{10,1... | collective-permute-start | bytes 1179656 | tf_op jit(solution)/shard_map/ppermute | solution.py:18
  183.3 19.4 %copy-start.4 = (f32[1,16384]{1,0:T(1,128)S(1)}, f32[1,16384]{1,0:T(1,128)}, u32[]{:S(2)}) copy-start(f32[1,16384]{1,0:T(1,128)} %get-tuple-element.10) | copy-start | bytes 196612
  239.3 1.6 copy-start.3
  255.8 8.8 %copy-start.1 = (f32[32,128,128]{2,1,0:T(8,128)}, f32[32,128,128]{2,1,0:T(8,128)S(1)}, u32[]{:S(2)}) copy-start(f32[32,128,128]{2,1,0:T(8,128)S(1)} %convolution_add_fusion) | copy-start | bytes 6291460
where the time goes:
time: 295 us; the launch traced here: 291 us
  other arithmetic  99.4 us (34%)
  matrix products  59.6 us (20%)
  waiting for transfers between devices  59.1 us (20%)
  local copies, waits for them, and re-layouts  37 us (13%)
  starting transfers between devices  34.7 us (12%)
    dot_general x16, matrix products, product(): return jnp.einsum(pattern, matrix, operand, precision=lax.Precision.HIGHEST)  59.6 us
    select_n x10, other arithmetic, kernel(): return jnp.where(inside, jnp.sinc(offsets) * tapering * tapering, 0.0)  54.9 us
    all_to_all x1, waiting for transfers between devices, per_device(): lax.all_to_all(blocks, 'row', split_axis=1, concat_axis=3, tiled=True)  42.8 us
    unnamed x2, other arithmetic  36.6 us
    all_to_all x1, starting transfers between devices, per_device(): lax.all_to_all(blocks, 'row', split_axis=1, concat_axis=3, tiled=True)  27.9 us
    ppermute x2, waiting for transfers between devices, from_behind(): return lax.ppermute(shard, axis, pairs)  16.3 us
    ppermute x2, starting transfers between devices, from_behind(): return lax.ppermute(shard, axis, pairs)  6.83 us
  transfers between devices with their start and end apart: 3, of which 2 were waited for; matrix products, arithmetic and copies ran while one was open for 21% of the time, Pallas kernels for 0%

commit v1 on v0

v1 whole, which is shorter than its diff:
```python
import math

import jax
import jax.numpy as jnp
import numpy as np
from jax import lax
from jax.experimental import pallas as pl
from jax.experimental.pallas import tpu as pltpu
from jax.sharding import PartitionSpec as P

FACTOR = 128
PULSES = 16384
BLOCK = 128
MAXSHIFT = 12
TAPS = 4
LOWER = TAPS - 1
UPPER = MAXSHIFT + TAPS - 1
COUNT = LOWER + UPPER + 1
PITCH = 72


def from_behind(shard, axis, by):
    devices = lax.axis_size(axis)
    pairs = [(i, i + by) for i in range(devices) if 0 <= i + by < devices]
    return lax.ppermute(shard, axis, pairs)


def split(values):
    high = values.astype(jnp.bfloat16)
    low = (values - high.astype(jnp.float32)).astype(jnp.bfloat16)
    return high, low


def tables():
    index = np.arange(FACTOR)
    product = index[:, None] * index[None, :]
    angle = 2.0 * np.pi / FACTOR * (product % FACTOR)
    c, s = np.cos(angle), np.sin(angle)
    left = np.block([[c, s], [-s, c]]).astype(np.float32)
    right = np.block([[c, -s], [s, c]]).astype(np.float32)
    twist = 2.0 * np.pi / PULSES * product
    pieces = []
    for matrix in (left, right):
        high = matrix.astype(jnp.bfloat16)
        low = (matrix - high.astype(np.float32)).astype(jnp.bfloat16)
        pieces += [jnp.asarray(high), jnp.asarray(low)]
    return pieces + [jnp.asarray(np.cos(twist), jnp.float32), jnp.asarray(np.sin(twist), jnp.float32)]


def dot3(a, b):
    def dot(x, y):
        return jnp.dot(x, y, preferred_element_type=jnp.float32)

    return dot(a[0], b[0]) + (dot(a[0], b[1]) + dot(a[1], b[0]))


def stack2(a, b, c, d):
    return jnp.concatenate([jnp.concatenate([a, b], axis=1), jnp.concatenate([c, d], axis=1)], axis=0)


def forward_body(x, lh, ll, rh, rl, tc, ts, spec, up, down, xs, sems):
    group = pl.program_id(0)
    groups = pl.num_programs(0)
    view = xs.reshape(FACTOR, PITCH, FACTOR)

    def fetch(g, part):
        rows = pl.ds(pl.multiple_of(8 * g, 8), 8)
        target = pl.ds(pl.multiple_of(32 * part + 8 * g, 8), 8)
        return pltpu.make_async_copy(x.at[:, part, rows, :], view.at[:, target, :], sems.at[g, part])

    @pl.when(group == 0)
    def _():
        for g in range(4):
            for part in range(2):
                fetch(g, part).start()

    for part in range(2):
        fetch(group, part).wait()

    def load(part, row):
        return xs[pl.ds(32 * part + row, FACTOR, stride=PITCH), :]

    def pair(row):
        data = stack2(load(0, row), load(0, row + 1), load(1, row), load(1, row + 1))
        first = dot3((lh[...], ll[...]), split(data))
        c, s = tc[...], ts[...]
        halves = []
        for i in range(2):
            fr = first[:FACTOR, FACTOR * i : FACTOR * (i + 1)]
            fi = first[FACTOR:, FACTOR * i : FACTOR * (i + 1)]
            halves.append((fr * c + fi * s, fi * c - fr * s))
        turned = stack2(halves[0][0], halves[0][1], halves[1][0], halves[1][1])
        return dot3(split(turned), (rh[...], rl[...]))

    def quad(step, carry):
        for half in range(2):
            local = 4 * step + 2 * half
            result = pair(8 * group + local)
            for i in range(2):
                for part in range(2):
                    value = result[FACTOR * i : FACTOR * (i + 1), FACTOR * part : FACTOR * (part + 1)]
                    spec[local + i, part] = value
                    row = 8 * group + local + i

                    @pl.when(row < UPPER)
                    def _():
                        up[row, part] = value

                    @pl.when(row >= 8 * groups - LOWER)
                    def _():
                        down[row - (8 * groups - LOWER), part] = value

        return carry

    lax.fori_loop(0, 2, quad, 0)


def forward(x, consts):
    rows = x.shape[2]
    whole = lambda shape: pl.BlockSpec(shape, lambda g: (0,) * len(shape))
    plane = (FACTOR, FACTOR)
    return pl.pallas_call(
        forward_body,
        grid=(rows // 8,),
        in_specs=[pl.BlockSpec(memory_space=pl.ANY)] + [whole((256, 256))] * 4 + [whole(plane)] * 2,
        out_specs=[
            pl.BlockSpec((8, 2) + plane, lambda g: (g, 0, 0, 0)),
            whole((UPPER, 2) + plane),
            whole((LOWER, 2) + plane),
        ],
        out_shape=[jax.ShapeDtypeStruct((n, 2) + plane, jnp.float32) for n in (rows, UPPER, LOWER)],
        scratch_shapes=[pltpu.VMEM((FACTOR * PITCH, FACTOR), jnp.float32), pltpu.SemaphoreType.DMA((4, 2))],
        compiler_params=pltpu.CompilerParams(vmem_limit_bytes=40 << 20),
        cost_estimate=pl.CostEstimate(flops=3 * 2 * 2 * 2 * 256 * 256 * 2048, bytes_accessed=10 << 20, transcendentals=0),
        name="forward",
    )(x, *consts)


def focus_body(spec, above, below, weights, chirp, lh, ll, rh, rl, tc, ts, out, ext, work, sems):
    group = pl.program_id(0)
    rows = spec.shape[0]
    copies = [
        pltpu.make_async_copy(spec, ext.at[pl.ds(LOWER, rows)], sems.at[0]),
        pltpu.make_async_copy(below, ext.at[pl.ds(0, LOWER)], sems.at[1]),
        pltpu.make_async_copy(above, ext.at[pl.ds(LOWER + rows, UPPER)], sems.at[2]),
    ]

    @pl.when(group == 0)
    def _():
        for copy in copies:
            copy.start()
        for copy in copies:
            copy.wait()

    view = out.reshape(2 * FACTOR * 8, FACTOR)

    def quad(step, carry):
        local = 4 * step
        base = 8 * group + local

        def tile(t, inner):
            sub = pl.ds(pl.multiple_of(8 * t, 8), 8)
            w = [weights[k, sub, :] for k in range(COUNT)]
            sums = [[None, None] for _ in range(4)]
            for j in range(COUNT + 3):
                values = [ext[base + j, part, sub, :] for part in range(2)]
                for i in range(4):
                    if 0 <= j - i < COUNT:
                        for part in range(2):
                            term = w[j - i] * values[part]
                            sums[i][part] = term if sums[i][part] is None else sums[i][part] + term
            for i in range(4):
                re, im = sums[i]
                c, s = chirp[local + i, 0, sub, :], chirp[local + i, 1, sub, :]
                target = pl.ds(pl.multiple_of(FACTOR * i + 8 * t, 8), 8)
                work[target, :FACTOR] = re * c + im * s
                work[target, FACTOR:] = im * c - re * s
            return inner

        lax.fori_loop(0, FACTOR // 8, tile, 0)
        for half in range(2):
            data = work[256 * half : 256 * (half + 1), :]
            first = dot3(split(data), (lh[...], ll[...]))
            c, s = tc[...], ts[...]
            halves = []
            for i in range(2):
                fr = first[FACTOR * i : FACTOR * (i + 1), :FACTOR]
                fi = first[FACTOR * i : FACTOR * (i + 1), FACTOR:]
                halves.append((fr * c - fi * s, fi * c + fr * s))
            turned = stack2(halves[0][0], halves[1][0], halves[0][1], halves[1][1])
            result = dot3((rh[...], rl[...]), split(turned))
            for i in range(2):
                for part in range(2):
                    value = result[FACTOR * part : FACTOR * (part + 1), FACTOR * i : FACTOR * (i + 1)]
                    view[pl.ds(FACTOR * 8 * part + local + 2 * half + i, FACTOR, stride=8), :] = value
        return carry

    lax.fori_loop(0, 2, quad, 0)


def focus(spec, above, below, weights, chirp, consts):
    rows = spec.shape[0]
    whole = lambda shape: pl.BlockSpec(shape, lambda g: (0,) * len(shape))
    plane = (FACTOR, FACTOR)
    anywhere = pl.BlockSpec(memory_space=pl.ANY)
    return pl.pallas_call(
        focus_body,
        grid=(rows // 8,),
        in_specs=[anywhere] * 3
        + [whole((COUNT,) + plane), pl.BlockSpec((8, 2) + plane, lambda g: (g, 0, 0, 0))]
        + [whole((256, 256))] * 4
        + [whole(plane)] * 2,
        out_specs=pl.BlockSpec((2, None, FACTOR, 8, FACTOR), lambda g: (0, g, 0, 0, 0)),
        out_shape=jax.ShapeDtypeStruct((2, rows // 8, FACTOR, 8, FACTOR), jnp.float32),
        scratch_shapes=[
            pltpu.VMEM((rows + LOWER + UPPER, 2) + plane, jnp.float32),
            pltpu.VMEM((512, 256), jnp.float32),
            pltpu.SemaphoreType.DMA((3,)),
        ],
        compiler_params=pltpu.CompilerParams(vmem_limit_bytes=40 << 20),
        cost_estimate=pl.CostEstimate(flops=3 * 2 * 2 * 2 * 256 * 256 * 2048, bytes_accessed=16 << 20, transcendentals=0),
        name="focus",
    )(spec, above, below, weights, chirp, *consts)


def spectral_tables(centroid, shifts, chirp_rate, own_rows):
    block = lax.axis_index("row") * own_rows // BLOCK
    chosen = block == jnp.arange(centroid.shape[0], dtype=jnp.int32)
    center = jnp.sum(jnp.where(chosen, centroid, 0))
    distance = jnp.sum(jnp.where(chosen, shifts, 0))
    index = jnp.arange(FACTOR, dtype=jnp.int32)
    bins = index[:, None] + FACTOR * index[None, :]
    wrapped = (bins - center + PULSES // 2) % PULSES - PULSES // 2
    relative = wrapped.astype(jnp.float32) / PULSES
    migration = distance.astype(jnp.float32) * 4.0 * relative * relative
    nearest = jnp.round(migration)
    sine = jnp.sin(math.pi * (migration - nearest)) / math.pi
    odd = nearest.astype(jnp.int32) % 2
    slow_cos, slow_sin = jnp.cos(math.pi / 4.0 * migration), jnp.sin(math.pi / 4.0 * migration)
    weights = []
    for offset in range(-LOWER, UPPER + 1):
        away = offset - migration
        sign = jnp.where((odd + offset) % 2 == 0, -1.0, 1.0)
        ratio = jnp.where(away == 0.0, 1.0, sign * sine / jnp.where(away == 0.0, 1.0, away))
        turn = math.pi / 4.0 * offset
        taper = 0.5 + 0.5 * (math.cos(turn) * slow_cos + math.sin(turn) * slow_sin)
        weights.append(jnp.where(jnp.abs(away) < TAPS, ratio * taper, 0.0))
    window = (0.54 + 0.46 * jnp.cos(2.0 * math.pi * relative)) / PULSES
    phase = math.pi * chirp_rate[:, None, None] * (relative * relative)
    return jnp.stack(weights), jnp.stack([window * jnp.cos(phase), window * jnp.sin(phase)], axis=1)


def per_device(raw_echo, centroid, shifts, chirp_rate):
    devices = lax.axis_size("row")
    own_rows = raw_echo.shape[1] // devices
    blocks = raw_echo.reshape(2, devices, own_rows, raw_echo.shape[2]).transpose(1, 0, 2, 3)
    received = lax.all_to_all(blocks, "row", split_axis=0, concat_axis=0, tiled=True)
    weights, chirp = spectral_tables(centroid, shifts, chirp_rate, own_rows)
    lh, ll, rh, rl, tc, ts = tables()
    spec, up, down = forward(received, (lh, ll, rh, rl, tc, ts))
    above = from_behind(up, "row", -1)
    below = from_behind(down, "row", 1)
    image = focus(spec, above, below, weights, chirp, (lh, ll, rh, rl, tc, ts))
    return image.transpose(0, 1, 3, 2, 4).reshape(2, own_rows, PULSES)


def solution(mesh):
    return jax.shard_map(
        per_device,
        mesh=mesh,
        in_specs=(P(None, "slab", "row"), P("slab"), P("slab"), P(("slab", "row"))),
        out_specs=P(None, ("slab", "row"), None),
        check_vma=False,
    )
```

time: 295 us -> 187 us (0.63); the launches traced: 291 us -> 187 us
  other arithmetic: 99.4 us -> 34.5 us
  matrix products: 59.6 us -> 0 us
  local copies, waits for them, and re-layouts: 37 us -> 4.9 us
  Pallas kernels: 0 us -> 28.6 us
  waiting for transfers between devices: 59.1 us -> 83.2 us
    dot_general x16 -> x0, matrix products: 59.6 us -> none  [product(): return jnp.einsum(pattern, matrix, operand, precision=lax.Precision.HIGHEST)]
    select_n x10 -> x0, other arithmetic: 54.9 us -> none  [kernel(): return jnp.where(inside, jnp.sinc(offsets) * tapering * tapering, 0.0)]
    all_to_all x1, waiting for transfers between devices: 42.8 us -> 78.4 us  [per_device(): lax.all_to_all(blocks, 'row', split_axis=0, concat_axis=0, tiled=True)]
    pallas_call x0 -> x2, Pallas kernels: none -> 28.6 us  [the longest x1 16.2 us: focus(): pl.pallas_call(focus_body, grid=(rows // 8,), in_specs=[anywhere] * 3 + [...]
    unnamed x2 -> x18, other arithmetic: 36.6 us -> 22.9 us
    ppermute x2, waiting for transfers between devices: 16.3 us -> 4.82 us  [from_behind(): return lax.ppermute(shard, axis, pairs)]
    another operation x5 -> x0, local copies, waits for them, and re-layouts: 8.92 us -> none  [the longest x3 4.62 us: spectral(): return jnp.stack(result)]
    mul x2 -> x3, other arithmetic: 0.65 us -> 7.46 us  [the longest x1 7.45 us: spectral_tables(): window * jnp.cos(phase)]
  transfers between devices with their start and end apart: 3 -> 3, of which waited for: 2 -> 3; matrix products, arithmetic and copies ran while one was open for 21% -> 18% of each run, Pallas kernels for 0% -> 0%
where the time goes in v1:
time: 187 us
  waiting for transfers between devices  83.2 us (44%)
  other arithmetic  34.5 us (18%)
  starting transfers between devices  34.4 us (18%)
  Pallas kernels  28.6 us (15%)
  local copies, waits for them, and re-layouts  4.9 us (3%)
    all_to_all x1, waiting for transfers between devices, per_device(): lax.all_to_all(blocks, 'row', split_axis=0, concat_axis=0, tiled=True)  78.4 us
    all_to_all x1, starting transfers between devices, per_device(): lax.all_to_all(blocks, 'row', split_axis=0, concat_axis=0, tiled=True)  27.3 us
    unnamed x18, other arithmetic  22.9 us
    pallas_call x1, Pallas kernels, focus(): pl.pallas_call(focus_body, grid=(rows // 8,), in_specs=[anywhere] * 3 + [...  16.2 us
    pallas_call x1, Pallas kernels, forward(): pl.pallas_call(forward_body, grid=(rows // 8,), in_specs=[pl.BlockSpec(me...  12.4 us
    mul x1, other arithmetic, spectral_tables(): window * jnp.cos(phase)  7.45 us
    ppermute x2, starting transfers between devices, from_behind(): return lax.ppermute(shard, axis, pairs)  7.05 us
    reshape x1, local copies, waits for them, and re-layouts, per_device(): raw_echo.reshape(2, devices, own_rows, raw_echo.shape[2])  4.85 us
  transfers between devices with their start and end apart: 3, of which 3 were waited for; matrix products, arithmetic and copies ran while one was open for 18% of the time, Pallas kernels for 0%

profile of v1, /device:TPU:519, one launch (start us, length us, event | category | flops | bytes accessed | tf_op | source)
XLA Modules:
  0.0 186.6 jit_solution(1002330864333053563)
XLA Ops:
  0.0 4.8 %copy.13 = f32[2,128,32,128]{3,2,0,1:T(8,128)} copy(f32[2,128,32,128]{3,2,1,0:T(8,128)} %bitcast.8) | data formatting | bytes 8388608 | tf_op jit(solution)/shard_map/reshape | solution.py:256
  4.9 27.3 %all-to-all-start = ((f32[128,2,32,128]{3,2,1,0:T(8,128)}), f32[128,2,32,128]{3,2,1,0:T(8,128)}, u32[]{:S(2)}, u32[]{:S(2)}) async-start(f32[128,2,32,128]{3,2,1,0:T(8,128)} %bitcast.7), calls=%async_computation | async-start | bytes 8388608 | tf_op jit(solution)/shard_map/all_to_all | solution.py:257
  32.2 0.0 copy-start
  32.2 0.0 copy-start.1
  32.2 0.0 copy-start.2
  32.2 0.0 copy-start.3
  32.2 0.0 copy-start.4
  32.2 0.0 copy-start.5
  32.3 0.0 copy-done.6
  32.3 0.7 fusion.128
  33.7 0.0 copy-done.7
  33.7 0.7 fusion.127
  34.4 1.3 fusion.5
  35.6 1.3 fusion.9
  36.9 1.3 fusion.13
  38.2 1.3 fusion.17
  39.5 1.3 fusion.21
  40.7 1.3 fusion.25
  42.0 1.3 fusion.29
  43.3 1.3 fusion.33
  44.5 1.3 fusion.37
  45.8 1.3 fusion.41
  47.1 1.3 fusion.45
  48.4 1.3 fusion.49
  49.6 1.3 fusion.53
  50.9 1.3 fusion.57
  52.2 0.0 copy-start.8
  52.2 78.4 %all-to-all-done.x = f32[128,2,32,128]{3,2,1,0:T(8,128)} async-done(((f32[128,2,32,128]{3,2,1,0:T(8,128)}), f32[128,2,32,128]{3,2,1,0:T(8,128)}, u32[]{:S(2)}, u32[]{:S(2)}) %all-to-all-start) | async-done | bytes 4194336 | tf_op jit(solution)/shard_map/all_to_all | solution.py:257
  130.6 0.0 copy-done
  130.6 0.0 copy-done.1
  130.6 0.0 copy-done.2
  130.6 0.0 copy-done.3
  130.6 0.0 copy-done.4
  130.6 12.4 %forward.1 = (f32[32,2,128,128]{3,2,1,0:T(8,128)S(1)}, f32[15,2,128,128]{3,2,1,0:T(8,128)S(1)}, f32[3,2,128,128]{3,2,1,0:T(8,128)S(1)}) custom-call(f32[128,2,32,128]{3,2,1,0:T(8,128)} %all-to-all-done.x, bf16[256,256]{1,0:T(8,128)(2,1)S(1)} %copy-done, bf16[256,256]{1,0:T(8,128)(2,1)S(1)} %copy-done.1, bf16[256,256]{1,0:T(8,128)(2,1)S(1)} %copy-done.2, ...), custom_call_target="tpu_custom_call" | custom-call | flops 3221225472 | bytes 10485760 | tf_op jit(solution)/shard_map/forward/pallas_call | solution.py:122
  143.1 3.4 %collective-permute-start = (f32[15,2,128,128]{3,2,1,0:T(8,128)S(1)}, f32[15,2,128,128]{3,2,1,0:T(8,128)S(1)}, u32[]{:S(2)}, u32[]{:S(2)}) collective-permute-start(f32[15,2,128,128]{3,2,1,0:T(8,128)S(1)} %get-tuple-element.9), channel_id=1, source_target_pairs={{1,0},{2,1},{3,2},{4,3},{5,4},{6,5},{7,6},{8,7},{9,8},{10,9},{11,1... | collective-permute-start | bytes 5898248 | tf_op jit(solution)/shard_map/ppermute | solution.py:25
  146.4 0.0 copy-done.8
  146.5 1.3 fusion.61
  147.7 1.3 fusion.65
  149.0 1.3 fusion.69
  150.3 1.3 fusion.73
  151.6 0.9 add_multiply_fusion
  152.5 7.5 %fusion = (f32[32,1,128,128]{3,2,1,0:T(8,128)S(1)}, f32[32,1,128,128]{3,2,1,0:T(8,128)S(1)}) fusion(f32[128,128]{1,0:T(8,128)S(1)} %get-tuple-element.14, f32[32]{0:T(128)S(1)} %broadcast_multiply_fusion, f32[128,128]{1,0:T(8,128)S(1)} %get-tuple-element.13), kind=kLoop, calls=%fused_computation.4 | loop fusion | flops 1572864 | bytes 4325504 | tf_op jit(solution)/shard_map/mul | solution.py:250
  160.0 3.7 %collective-permute-start.1 = (f32[3,2,128,128]{3,2,1,0:T(8,128)S(1)}, f32[3,2,128,128]{3,2,1,0:T(8,128)S(1)}, u32[]{:S(2)}, u32[]{:S(2)}) collective-permute-start(f32[3,2,128,128]{3,2,1,0:T(8,128)S(1)} %get-tuple-element.10), channel_id=1, source_target_pairs={{0,1},{1,2},{2,3},{3,4},{4,5},{5,6},{6,7},{7,8},{8,9},{9,10},{10,1... | collective-permute-start | bytes 1179656 | tf_op jit(solution)/shard_map/ppermute | solution.py:25
  163.7 0.5 pad_maximum_fusion.chirp
  164.2 1.3 fusion.77.weights
  165.4 2.9 %collective-permute-done.1.below = f32[3,2,128,128]{3,2,1,0:T(8,128)S(1)} collective-permute-done((f32[3,2,128,128]{3,2,1,0:T(8,128)S(1)}, f32[3,2,128,128]{3,2,1,0:T(8,128)S(1)}, u32[]{:S(2)}, u32[]{:S(2)}) %collective-permute-start.1) | collective-permute-done | bytes 393248 | tf_op jit(solution)/shard_map/ppermute | solution.py:25
  168.4 1.9 %collective-permute-done.above = f32[15,2,128,128]{3,2,1,0:T(8,128)S(1)} collective-permute-done((f32[15,2,128,128]{3,2,1,0:T(8,128)S(1)}, f32[15,2,128,128]{3,2,1,0:T(8,128)S(1)}, u32[]{:S(2)}, u32[]{:S(2)}) %collective-permute-start) | collective-permute-done | bytes 1966112 | tf_op jit(solution)/shard_map/ppermute | solution.py:25
  170.3 16.2 %focus.1 = f32[2,4,128,8,128]{4,3,2,1,0:T(8,128)} custom-call(f32[32,2,128,128]{3,2,1,0:T(8,128)S(1)} %get-tuple-element.8.spec, f32[15,2,128,128]{3,2,1,0:T(8,128)S(1)} %collective-permute-done.above, f32[3,2,128,128]{3,2,1,0:T(8,128)S(1)} %collective-permute-done.1.below, f32[19,128,128]{2,1,0:T(8,128)S(1)} %fusion.77.weights, ...), custom_call_target="tpu_custom_call" | custom-call | flops 3221225472 | bytes 16777216 | tf_op jit(solution)/shard_map/focus/pallas_call | solution.py:206
  (5 shorter events, 0.0 us)
Async XLA Ops:
  4.8 27.4 %copy-start.6 = (s32[32]{0:T(128)S(1)}, s32[32]{0:T(128)}, u32[]{:S(2)}) copy-start(s32[32]{0:T(128)} %param.12) | copy-start | bytes 388
  4.8 28.8 %copy-start.7 = (s32[32]{0:T(128)S(1)}, s32[32]{0:T(128)}, u32[]{:S(2)}) copy-start(s32[32]{0:T(128)} %param.11) | copy-start | bytes 388
  4.9 125.7 %all-to-all-start = ((f32[128,2,32,128]{3,2,1,0:T(8,128)}), f32[128,2,32,128]{3,2,1,0:T(8,128)}, u32[]{:S(2)}, u32[]{:S(2)}) async-start(f32[128,2,32,128]{3,2,1,0:T(8,128)} %bitcast.7), calls=%async_computation | async-start | bytes 8388608 | tf_op jit(solution)/shard_map/all_to_all | solution.py:257
  32.2 98.4 %copy-start = (bf16[256,256]{1,0:T(8,128)(2,1)S(1)}, bf16[256,256]{1,0:T(8,128)(2,1)}, u32[]{:S(2)}) copy-start(bf16[256,256]{1,0:T(8,128)(2,1)} %constant.275.clone.lh) | copy-start | bytes 393220
  32.2 98.4 %copy-start.1 = (bf16[256,256]{1,0:T(8,128)(2,1)S(1)}, bf16[256,256]{1,0:T(8,128)(2,1)}, u32[]{:S(2)}) copy-start(bf16[256,256]{1,0:T(8,128)(2,1)} %constant.276.clone.ll) | copy-start | bytes 393220
  32.2 98.4 %copy-start.2 = (bf16[256,256]{1,0:T(8,128)(2,1)S(1)}, bf16[256,256]{1,0:T(8,128)(2,1)}, u32[]{:S(2)}) copy-start(bf16[256,256]{1,0:T(8,128)(2,1)} %constant.277.clone.rh) | copy-start | bytes 393220
  32.2 98.4 %copy-start.3 = (bf16[256,256]{1,0:T(8,128)(2,1)S(1)}, bf16[256,256]{1,0:T(8,128)(2,1)}, u32[]{:S(2)}) copy-start(bf16[256,256]{1,0:T(8,128)(2,1)} %constant.278.clone.rl) | copy-start | bytes 393220
  32.2 98.4 %copy-start.4 = (f32[128,128]{1,0:T(8,128)S(1)}, f32[128,128]{1,0:T(8,128)}, u32[]{:S(2)}) copy-start(f32[128,128]{1,0:T(8,128)} %constant.279.clone.tc) | copy-start | bytes 196612
  32.2 98.4 %copy-start.5 = (f32[128,128]{1,0:T(8,128)S(1)}, f32[128,128]{1,0:T(8,128)}, u32[]{:S(2)}) copy-start(f32[128,128]{1,0:T(8,128)} %constant.280.clone.ts) | copy-start | bytes 196612
  52.2 94.3 %copy-start.8 = (f32[32]{0:T(128)S(1)}, f32[32]{0:T(128)}, u32[]{:S(2)}) copy-start(f32[32]{0:T(128)} %param.13) | copy-start | bytes 388
  143.1 27.2 %collective-permute-start = (f32[15,2,128,128]{3,2,1,0:T(8,128)S(1)}, f32[15,2,128,128]{3,2,1,0:T(8,128)S(1)}, u32[]{:S(2)}, u32[]{:S(2)}) collective-permute-start(f32[15,2,128,128]{3,2,1,0:T(8,128)S(1)} %get-tuple-element.9), channel_id=1, source_target_pairs={{1,0},{2,1},{3,2},{4,3},{5,4},{6,5},{7,6},{8,7},{9,8},{10,9},{11,1... | collective-permute-start | bytes 5898248 | tf_op jit(solution)/shard_map/ppermute | solution.py:25
  160.0 8.4 %collective-permute-start.1 = (f32[3,2,128,128]{3,2,1,0:T(8,128)S(1)}, f32[3,2,128,128]{3,2,1,0:T(8,128)S(1)}, u32[]{:S(2)}, u32[]{:S(2)}) collective-permute-start(f32[3,2,128,128]{3,2,1,0:T(8,128)S(1)} %get-tuple-element.10), channel_id=1, source_target_pairs={{0,1},{1,2},{2,3},{3,4},{4,5},{5,6},{6,7},{7,8},{8,9},{9,10},{10,1... | collective-permute-start | bytes 1179656 | tf_op jit(solution)/shard_map/ppermute | solution.py:25

commit v2 on v0

v2 whole, which is shorter than its diff:
```python
import math

import jax
import jax.numpy as jnp
from jax import lax
from jax.experimental import pallas as pl
from jax.experimental.pallas import tpu as pltpu
from jax.sharding import PartitionSpec as P

FACTOR = 128
PULSES = 16384
BLOCK = 128
MAXSHIFT = 12
TAPS = 4
LOWER = TAPS - 1
UPPER = MAXSHIFT + TAPS - 1
PITCH = 72
TILES = FACTOR // 8
PLANE = (FACTOR, FACTOR)
TABLE = (2 * FACTOR, 2 * FACTOR)


def edge(tile):
    return min(tile, TILES - 1 - tile)


def last_tap(tile):
    return math.ceil(4 * MAXSHIFT * ((8 - edge(tile)) / TILES) ** 2) + TAPS - 1


def tap_count(tile):
    near, far = (7 - edge(tile)) / TILES, (8 - edge(tile)) / TILES
    return max(math.ceil(4 * s * far**2) - math.floor(4 * s * near**2) + 2 * TAPS - 1 for s in range(MAXSHIFT + 1))


def side_tiles(row):
    return sum(4 * MAXSHIFT * ((8 - e) / TILES) ** 2 > row - LOWER for e in range(TILES // 2))


COUNTS = [tap_count(t) for t in range(TILES)]
LASTS = [last_tap(t) for t in range(TILES)]
SIDES = [side_tiles(j) for j in range(UPPER)]
STARTS = [16 * sum(SIDES[:j]) for j in range(UPPER + 1)]


def from_behind(shard, axis, by):
    devices = lax.axis_size(axis)
    pairs = [(i, i + by) for i in range(devices) if 0 <= i + by < devices]
    return lax.ppermute(shard, axis, pairs)


def split(values):
    high = values.astype(jnp.bfloat16)
    low = (values - high.astype(jnp.float32)).astype(jnp.bfloat16)
    return high, low


def stack2(a, b, c, d):
    return jnp.concatenate([jnp.concatenate([a, b], axis=1), jnp.concatenate([c, d], axis=1)], axis=0)


def multiply(table, data, across):
    dims = (((1,), (1 if across else 0,)), ((), ()))

    def dot(x, y):
        return lax.dot_general(x, y, dims, preferred_element_type=jnp.float32)

    high, low = split(data)
    return dot(table[0][...], high) + (dot(table[0][...], low) + dot(table[1][...], high))


def quarters(values):
    n = FACTOR
    return values[:n, :n], values[:n, n:], values[n:, :n], values[n:, n:]


def transform_pair(re0, re1, im0, im1, first, twist, second, sign):
    a = multiply(first, stack2(re0, re1, im0, im1), False)
    r0, r1, i0, i1 = quarters(a)
    c, s = twist[0][...], twist[1][...]
    if sign < 0:
        turned = stack2(r0 * c + i0 * s, i0 * c - r0 * s, r1 * c + i1 * s, i1 * c - r1 * s)
    else:
        turned = stack2(r0 * c - i0 * s, i0 * c + r0 * s, r1 * c - i1 * s, i1 * c + r1 * s)
    return quarters(multiply(second, turned, True))


def fetcher(x, xs, sems):
    view = xs.reshape(FACTOR, PITCH, FACTOR)

    def fetch(g, part):
        rows = pl.ds(pl.multiple_of(8 * g, 8), 8)
        target = pl.ds(pl.multiple_of(32 * part + 8 * g, 8), 8)
        return pltpu.make_async_copy(x.at[:, part, rows, :], view.at[:, target, :], sems.at[g, part])

    return fetch


def forward_pair(xs, row, tables):
    def load(part, r):
        return xs[pl.ds(32 * part + r, FACTOR, stride=PITCH), :]

    return transform_pair(
        load(0, row), load(0, row + 1), load(1, row), load(1, row + 1), tables[0:2], tables[2:4], tables[4:6], -1
    )


def halo_body(*refs):
    x, up_tables, down_tables = refs[0], refs[1:7], refs[7:13]
    up, down, xs, sems = refs[13:]
    fetch = fetcher(x, xs, sems)
    for g in (0, 1, 3):
        for part in range(2):
            fetch(g, part).start()
    for g in (0, 1, 3):
        for part in range(2):
            fetch(g, part).wait()
        for row in range(8 * g, 8 * g + 8, 2):
            if g < 3:
                re0, re1, im0, im1 = forward_pair(xs, row, up_tables)
                for r, re, im in ((row, re0, im0), (row + 1, re1, im1)):
                    if r < UPPER:
                        start, size = STARTS[r], 8 * SIDES[r]
                        for part, value in enumerate((re, im)):
                            up[part, start : start + size, :] = value[:size]
                            up[part, start + size : start + 2 * size, :] = value[FACTOR - size :]
            elif row + 1 >= 32 - LOWER:
                re0, re1, im0, im1 = forward_pair(xs, row, down_tables)
                for r, re, im in ((row, re0, im0), (row + 1, re1, im1)):
                    if r >= 32 - LOWER:
                        down[r - 32 + LOWER, 0] = re
                        down[r - 32 + LOWER, 1] = im


def halo(x, up_tables, down_tables):
    return pl.pallas_call(
        halo_body,
        in_specs=[pl.BlockSpec(memory_space=pl.ANY)] + [pl.BlockSpec(memory_space=pltpu.VMEM)] * 12,
        out_shape=[
            jax.ShapeDtypeStruct((2, STARTS[-1], FACTOR), jnp.float32),
            jax.ShapeDtypeStruct((LOWER, 2) + PLANE, jnp.float32),
        ],
        scratch_shapes=[pltpu.VMEM((FACTOR * PITCH, FACTOR), jnp.float32), pltpu.SemaphoreType.DMA((4, 2))],
        compiler_params=pltpu.CompilerParams(vmem_limit_bytes=16 << 20),
        cost_estimate=pl.CostEstimate(flops=5 << 30, bytes_accessed=5 << 20, transcendentals=0),
        name="halo",
    )(x, *up_tables, *down_tables)


def forward_body(*refs):
    x, tables = refs[0], refs[1:7]
    spec, xs, sems = refs[7:]
    group = pl.program_id(0)
    fetch = fetcher(x, xs, sems)

    @pl.when(group == 0)
    def _():
        for g in range(4):
            for part in range(2):
                fetch(g, part).start()

    for part in range(2):
        fetch(group, part).wait()
    for local in range(0, 8, 2):
        re0, re1, im0, im1 = forward_pair(xs, 8 * group + local, tables)
        spec[local, 0] = re0
        spec[local + 1, 0] = re1
        spec[local, 1] = im0
        spec[local + 1, 1] = im1


def whole(shape):
    return pl.BlockSpec(shape, lambda *_: (0,) * len(shape))


def forward(x, tables):
    rows = x.shape[2]
    return pl.pallas_call(
        forward_body,
        grid=(rows // 8,),
        in_specs=[pl.BlockSpec(memory_space=pl.ANY)] + [whole(t.shape) for t in tables],
        out_specs=pl.BlockSpec((8, 2) + PLANE, lambda g: (g, 0, 0, 0)),
        out_shape=jax.ShapeDtypeStruct((rows, 2) + PLANE, jnp.float32),
        scratch_shapes=[pltpu.VMEM((FACTOR * PITCH, FACTOR), jnp.float32), pltpu.SemaphoreType.DMA((4, 2))],
        compiler_params=pltpu.CompilerParams(vmem_limit_bytes=16 << 20),
        cost_estimate=pl.CostEstimate(flops=8 << 30, bytes_accessed=8 << 20, transcendentals=0),
        name="forward",
    )(x, *tables)


def focus_rows(ext, taps, weights, chirp, tables, view, base, local):
    tiles = [[[], []] for _ in range(4)]
    for t in range(TILES):
        sub = slice(8 * t, 8 * t + 8)
        start = base + local + taps[t] + LOWER
        w = [weights[k, sub, :] for k in range(COUNTS[t])]
        sums = [[None, None] for _ in range(4)]
        for j in range(COUNTS[t] + 3):
            values = [ext[start + j, part, sub, :] for part in range(2)]
            for i in range(4):
                if 0 <= j - i < COUNTS[t]:
                    for part in range(2):
                        term = w[j - i] * values[part]
                        sums[i][part] = term if sums[i][part] is None else sums[i][part] + term
        for i in range(4):
            re, im = sums[i]
            c, s = chirp[local + i, 0, sub, :], chirp[local + i, 1, sub, :]
            tiles[i][0].append(re * c + im * s)
            tiles[i][1].append(im * c - re * s)
    planes = [[jnp.concatenate(part, axis=0) for part in row] for row in tiles]
    for i in (0, 2):
        (re0, im0), (re1, im1) = planes[i], planes[i + 1]
        re0, re1, im0, im1 = transform_pair(re0, re1, im0, im1, tables[0:2], tables[2:4], tables[4:6], 1)
        for part, r, value in ((0, 0, re0), (0, 1, re1), (1, 0, im0), (1, 1, im1)):
            view[pl.ds(FACTOR * 8 * part + local + i + r, FACTOR, stride=8), :] = value


def inner_body(*refs):
    taps, spec, weights, chirp = refs[:4]
    tables, (out, ext, sems) = refs[4:10], refs[10:]
    first, count = 8 - LOWER, 8 + LOWER + UPPER
    copy = pltpu.make_async_copy(spec.at[pl.ds(first, count)], ext.at[pl.ds(8, count)], sems.at[0])
    copy.start()
    copy.wait()
    view = out.reshape(2 * FACTOR * 8, FACTOR)
    for local in (0, 4):
        focus_rows(ext, taps, weights, chirp, tables, view, 8, local)


def outer_body(*refs):
    taps, spec, up, down, weights, chirp = refs[:6]
    tables, (_, out, ext, sems) = refs[6:12], refs[12:]
    step = pl.program_id(0)
    rows = spec.shape[0]

    @pl.when(step == 0)
    def _():
        copy = pltpu.make_async_copy(spec, ext.at[pl.ds(LOWER, rows)], sems.at[0])
        copy.start()
        for r in range(LOWER):
            ext[r] = down[r]
        for r in range(UPPER):
            start, size = STARTS[r], 8 * SIDES[r]
            for part in range(2):
                ext[LOWER + rows + r, part, :size, :] = up[part, start : start + size, :]
                ext[LOWER + rows + r, part, FACTOR - size :, :] = up[part, start + size : start + 2 * size, :]
        copy.wait()

    view = out.reshape(2 * FACTOR * 8, FACTOR)
    base = 8 * (step + jnp.minimum(step, 1))
    for local in (0, 4):
        focus_rows(ext, taps, weights, chirp, tables, view, base, local)


def focus(group_of, steps, body, taps, operands, kinds, weights, chirp, tables, rows, prior, name):
    chunk = lambda g: (group_of(g), 0, 0, 0)
    image = pl.BlockSpec((2, None, FACTOR, 8, FACTOR), lambda g: (0, group_of(g), 0, 0, 0))
    specs = [pl.BlockSpec(memory_space=pltpu.SMEM)] + kinds + [whole(weights.shape), pl.BlockSpec((8, 2) + PLANE, chunk)]
    specs += [whole(t.shape) for t in tables]
    args = [taps, *operands, weights, chirp, *tables]
    aliases = {}
    if prior is not None:
        aliases = {len(args): 0}
        specs.append(pl.BlockSpec(memory_space=pl.ANY))
        args.append(prior)
    return pl.pallas_call(
        body,
        grid=(steps,),
        in_specs=specs,
        out_specs=image,
        out_shape=jax.ShapeDtypeStruct((2, rows // 8, FACTOR, 8, FACTOR), jnp.float32),
        input_output_aliases=aliases,
        scratch_shapes=[
            pltpu.VMEM((rows + LOWER + UPPER, 2) + PLANE, jnp.float32),
            pltpu.SemaphoreType.DMA((1,)),
        ],
        compiler_params=pltpu.CompilerParams(vmem_limit_bytes=24 << 20),
        cost_estimate=pl.CostEstimate(flops=steps * (3 << 30), bytes_accessed=steps * (4 << 20), transcendentals=0),
        name=name,
    )(*args)


def two_parts(values):
    high = lax.reduce_precision(values, 8, 7)
    return high.astype(jnp.bfloat16), (values - high).astype(jnp.bfloat16)


def turns(product, modulus):
    angle = 2.0 * math.pi / modulus * (product % modulus).astype(jnp.float32)
    return jnp.cos(angle), jnp.sin(angle)


def transform_tables(center, sign):
    start = (center - PULSES // 2) % PULSES
    index = jnp.arange(FACTOR, dtype=jnp.int32)
    fine, coarse = index + start % FACTOR, index + start // FACTOR

    def block(a, b):
        c, s = turns(a[:, None] * b[None, :], FACTOR)
        return two_parts(stack2(c, -sign * s, sign * s, c))

    if sign < 0:
        twist = turns(fine[:, None] * index[None, :], PULSES)
        return [*block(fine, index), *twist, *block(coarse, index)]
    twist = turns(index[:, None] * fine[None, :], PULSES)
    return [*block(index, coarse), *twist, *block(index, fine)]


def spectral_tables(distance, chirp_rate):
    index = jnp.arange(FACTOR, dtype=jnp.int32)
    bins = FACTOR * index[:, None] + index[None, :]
    relative = (bins - PULSES // 2).astype(jnp.float32) / PULSES
    migration = distance.astype(jnp.float32) * 4.0 * relative * relative
    nearness = jnp.array([(7 - edge(t)) ** 2 for t in range(TILES)], jnp.int32)
    latest = jnp.array([LASTS[t] - COUNTS[t] + 1 for t in range(TILES)], jnp.int32)
    taps = jnp.minimum(distance * nearness // (TILES * TILES // 4) - LOWER, latest)
    nearest = jnp.round(migration)
    sine = jnp.sin(math.pi * (migration - nearest)) / math.pi
    quarter = math.pi / TAPS
    offset = jnp.repeat(taps, 8)[None, :, None] + jnp.arange(max(COUNTS), dtype=jnp.int32)[:, None, None]
    away = offset.astype(jnp.float32) - migration
    sign = jnp.where((nearest.astype(jnp.int32) + offset) % 2 == 0, -1.0, 1.0)
    ratio = jnp.where(away == 0.0, 1.0, sign * sine / jnp.where(away == 0.0, 1.0, away))
    inside = jnp.abs(away) < TAPS
    weights = jnp.where(inside, ratio * (0.5 + 0.5 * jnp.cos(quarter * away)), 0.0)
    window = (0.54 + 0.46 * jnp.cos(2.0 * math.pi * relative)) / PULSES
    phase = math.pi * chirp_rate[:, None, None] * (relative * relative)
    return taps, weights, jnp.stack([window * jnp.cos(phase), window * jnp.sin(phase)], axis=1)


def compute(received, exchange, own, below, above, distance, chirp_rate):
    rows = received.shape[2]
    taps, weights, chirp = spectral_tables(distance, chirp_rate)
    inverse = transform_tables(own, 1)
    up, down = halo(received, transform_tables(below, -1), transform_tables(above, -1))
    up, down = exchange(up, down)
    spec = forward(received, transform_tables(own, -1))
    anywhere = pl.BlockSpec(memory_space=pl.ANY)
    image = focus(lambda g: 1, 1, inner_body, taps, [spec], [anywhere], weights, chirp, inverse, rows, None, "inner")
    kinds = [anywhere, whole(up.shape), whole(down.shape)]
    later = lambda g: g + jnp.minimum(g, 1)
    image = focus(later, 3, outer_body, taps, [spec, up, down], kinds, weights, chirp, inverse, rows, image, "outer")
    return image.transpose(0, 1, 3, 2, 4).reshape(2, rows, PULSES)


def per_device(raw_echo, centroid, shifts, chirp_rate):
    devices = lax.axis_size("row")
    own_rows = raw_echo.shape[1] // devices
    blocks = raw_echo.reshape(2, devices, own_rows, raw_echo.shape[2]).transpose(1, 0, 2, 3)
    received = lax.all_to_all(blocks, "row", split_axis=0, concat_axis=0, tiled=True)

    def pick(values, device):
        block = jnp.clip(device, 0, devices - 1) * own_rows // BLOCK
        return jnp.sum(jnp.where(block == jnp.arange(values.shape[0], dtype=jnp.int32), values, 0))

    def exchange(up, down):
        return from_behind(up, "row", -1), from_behind(down, "row", 1)

    device = lax.axis_index("row")
    centers = [pick(centroid, device + by) for by in (0, -1, 1)]
    return compute(received, exchange, *centers, pick(shifts, device), chirp_rate)


def solution(mesh):
    return jax.shard_map(
        per_device,
        mesh=mesh,
        in_specs=(P(None, "slab", "row"), P("slab"), P("slab"), P(("slab", "row"))),
        out_specs=P(None, ("slab", "row"), None),
        check_vma=False,
    )
```

time: 295 us -> 165 us (0.56); the launches traced: 291 us -> 165 us
  other arithmetic: 99.4 us -> 19.3 us
  matrix products: 59.6 us -> 0 us
  local copies, waits for them, and re-layouts: 37 us -> 5.03 us
  Pallas kernels: 0 us -> 24.9 us
  waiting for transfers between devices: 59.1 us -> 79.8 us
    dot_general x16 -> x0, matrix products: 59.6 us -> none  [product(): return jnp.einsum(pattern, matrix, operand, precision=lax.Precision.HIGHEST)]
    select_n x10 -> x1, other arithmetic: 54.9 us -> 3 us  [spectral_tables(): jnp.where(inside, ratio * (0.5 + 0.5 * jnp.cos(quarter * away)), 0.0)]
    unnamed x2 -> x0, other arithmetic: 36.6 us -> none
    all_to_all x1, waiting for transfers between devices: 42.8 us -> 75.5 us  [per_device(): lax.all_to_all(blocks, 'row', split_axis=0, concat_axis=0, tiled=True)]
    pallas_call x0 -> x4, Pallas kernels: none -> 24.9 us  [the longest x2 12.5 us: focus(): pl.pallas_call(body, grid=(steps,), in_specs=specs, out_specs=image, out_...]
    ppermute x2, waiting for transfers between devices: 16.3 us -> 4.24 us  [from_behind(): return lax.ppermute(shard, axis, pairs)]
    another operation x5 -> x0, local copies, waits for them, and re-layouts: 8.92 us -> none  [the longest x3 4.62 us: spectral(): return jnp.stack(result)]
    mul x2 -> x5, other arithmetic: 0.65 us -> 9.28 us  [the longest x1 7.68 us: spectral_tables(): window * jnp.cos(phase)]
  transfers between devices with their start and end apart: 3 -> 3, of which waited for: 2 -> 2; matrix products, arithmetic and copies ran while one was open for 21% -> 12% of each run, Pallas kernels for 0% -> 7%
where the time goes in v2:
time: 165 us
  waiting for transfers between devices  79.8 us (48%)
  starting transfers between devices  32.9 us (20%)
  Pallas kernels  24.9 us (15%)
  other arithmetic  19.3 us (12%)
  local copies, waits for them, and re-layouts  5.03 us (3%)
  between operations  3.22 us (2%)
    all_to_all x1, waiting for transfers between devices, per_device(): lax.all_to_all(blocks, 'row', split_axis=0, concat_axis=0, tiled=True)  75.5 us
    all_to_all x1, starting transfers between devices, per_device(): lax.all_to_all(blocks, 'row', split_axis=0, concat_axis=0, tiled=True)  27.5 us
    pallas_call x2, Pallas kernels, focus(): pl.pallas_call(body, grid=(steps,), in_specs=specs, out_specs=image, out_...  12.5 us
    mul x1, other arithmetic, spectral_tables(): window * jnp.cos(phase)  7.68 us
    pallas_call x1, Pallas kernels, forward(): pl.pallas_call(forward_body, grid=(rows // 8,), in_specs=[pl.BlockSpec(me...  7.33 us
    ppermute x2, starting transfers between devices, from_behind(): return lax.ppermute(shard, axis, pairs)  5.44 us
    pallas_call x1, Pallas kernels, halo(): pl.pallas_call(halo_body, in_specs=[pl.BlockSpec(memory_space=pl.ANY)] +...  5.04 us
    reshape x1, local copies, waits for them, and re-layouts, per_device(): raw_echo.reshape(2, devices, own_rows, raw_echo.shape[2])  4.85 us
  transfers between devices with their start and end apart: 3, of which 2 were waited for; matrix products, arithmetic and copies ran while one was open for 12% of the time, Pallas kernels for 7%

profile of v2, /device:TPU:519, one launch (start us, length us, event | category | flops | bytes accessed | tf_op | source)
XLA Modules:
  0.0 165.1 jit_solution(13415350333714976058)
XLA Ops:
  0.0 4.8 %copy.10 = f32[2,128,32,128]{3,2,0,1:T(8,128)} copy(f32[2,128,32,128]{3,2,1,0:T(8,128)} %bitcast.8) | data formatting | bytes 8388608 | tf_op jit(solution)/shard_map/reshape | solution.py:349
  4.8 0.0 copy-start.1
  4.8 0.0 copy-start.4
  4.9 0.0 copy-start.2
  4.9 0.0 copy-start.3
  4.9 27.5 %all-to-all-start = ((f32[128,2,32,128]{3,2,1,0:T(8,128)}), f32[128,2,32,128]{3,2,1,0:T(8,128)}, u32[]{:S(2)}, u32[]{:S(2)}) async-start(f32[128,2,32,128]{3,2,1,0:T(8,128)} %bitcast.7), calls=%async_computation | async-start | bytes 8388608 | tf_op jit(solution)/shard_map/all_to_all | solution.py:350
  32.4 0.0 copy-done.1
  32.4 0.7 fusion.120
  35.0 0.0 copy-done.4
  35.0 0.7 fusion.117
  36.5 0.0 copy-done.2
  36.5 0.0 copy-done.3
  36.5 0.7 add_minimum_fusion.refs_0_
  37.2 0.1 broadcast_in_dim.23
  37.2 0.1 add.306
  37.5 0.3 fusion.98
  37.8 0.6 fusion.100
  38.4 0.1 fusion.16
  38.5 0.3 fusion.104
  38.8 0.0 copy-start.5
  38.8 0.6 fusion.106
  39.4 0.1 fusion.14
  39.5 0.6 broadcast_multiply_fusion.1
  40.1 1.0 broadcast_multiply_fusion
  41.1 0.1 fusion.18
  41.2 0.1 fusion.12
  41.3 0.0 copy-done.5
  41.3 0.5 add_multiply_fusion
  41.8 7.7 %fusion = (f32[32,1,128,128]{3,2,1,0:T(8,128)S(1)}, f32[32,1,128,128]{3,2,1,0:T(8,128)S(1)}) fusion(f32[128,128]{1,0:T(8,128)S(1)} %get-tuple-element.49, f32[32]{0:T(128)S(1)} %broadcast_multiply_fusion.8, f32[128,128]{1,0:T(8,128)S(1)} %get-tuple-element.46), kind=kLoop, calls=%fused_computation.4 | loop fusion | flops 1572864 | bytes 4325504 | tf_op jit(solution)/shard_map/mul | solution.py:328
  49.5 2.2 %pad_maximum_fusion.refs_3_.refs_5_ = f32[32,2,128,128]{3,2,1,0:T(8,128)} fusion(f32[32,1,128,128]{3,2,1,0:T(8,128)S(1)} %get-tuple-element.29, f32[32,1,128,128]{3,2,1,0:T(8,128)S(1)} %get-tuple-element.28), kind=kLoop, calls=%fused_computation | loop fusion | flops 1048576 | bytes 8388608 | tf_op jit(solution)/shard_map/stack | solution.py:328
  51.8 3.0 %fusion.4.refs_2_.refs_4_ = f32[11,128,128]{2,1,0:T(8,128)S(1)} fusion(f32[128,128]{1,0:T(8,128)S(1)} %get-tuple-element.48, s32[11,128]{1,0:T(8,128)S(1)} %get-tuple-element.52, s32[128,128]{1,0:T(8,128)S(1)} %get-tuple-element.47, f32[128,128]{1,0:T(8,128)S(1)} %get-tuple-element.50, f32[11,128]{1,0:T(8,128)S(1)} %get-tuple-element.51), kind=kLoop, calls=%fused_computation.17 | loop fusion | flops 4866048 | bytes 928768 | tf_op jit(solution)/shard_map/jit(_where)/select_n | solution.py:325
  54.8 75.5 %all-to-all-done.refs_0_ = f32[128,2,32,128]{3,2,1,0:T(8,128)} async-done(((f32[128,2,32,128]{3,2,1,0:T(8,128)}), f32[128,2,32,128]{3,2,1,0:T(8,128)}, u32[]{:S(2)}, u32[]{:S(2)}) %all-to-all-start) | async-done | bytes 4194336 | tf_op jit(solution)/shard_map/all_to_all | solution.py:350
  130.3 5.0 %halo.1 = (f32[2,1040,128]{2,1,0:T(8,128)S(1)}, f32[3,2,128,128]{3,2,1,0:T(8,128)S(1)}) custom-call(f32[128,2,32,128]{3,2,1,0:T(8,128)} %all-to-all-done.refs_0_, bf16[256,256]{1,0:T(8,128)(2,1)S(1)} %get-tuple-element.23.refs_1_, bf16[256,256]{1,0:T(8,128)(2,1)S(1)} %get-tuple-element.22.refs_2_, f32[128,128]{1,0:T(8,128)S(1)} %get-tuple-element.68.refs_3_, ...), custom_call_target="tpu_custom_call" | custom-call | flops 5368709120 | bytes 5242880 | tf_op jit(solution)/shard_map/halo/pallas_call | solution.py:136
  135.3 3.5 %collective-permute-start.1 = (f32[3,2,128,128]{3,2,1,0:T(8,128)S(1)}, f32[3,2,128,128]{3,2,1,0:T(8,128)S(1)}, u32[]{:S(2)}, u32[]{:S(2)}) collective-permute-start(f32[3,2,128,128]{3,2,1,0:T(8,128)S(1)} %get-tuple-element.8), channel_id=1, source_target_pairs={{0,1},{1,2},{2,3},{3,4},{4,5},{5,6},{6,7},{7,8},{8,9},{9,10},{10,1... | collective-permute-start | bytes 1179656 | tf_op jit(solution)/shard_map/ppermute | solution.py:49
  138.8 2.0 %collective-permute-start = (f32[2,1040,128]{2,1,0:T(8,128)S(1)}, f32[2,1040,128]{2,1,0:T(8,128)S(1)}, u32[]{:S(2)}, u32[]{:S(2)}) collective-permute-start(f32[2,1040,128]{2,1,0:T(8,128)S(1)} %get-tuple-element.7), channel_id=1, source_target_pairs={{1,0},{2,1},{3,2},{4,3},{5,4},{6,5},{7,6},{8,7},{9,8},{10,9},{11,1... | collective-permute-start | bytes 3194888 | tf_op jit(solution)/shard_map/ppermute | solution.py:49
  140.8 0.0 copy-start
  140.8 7.3 %forward.1.refs_1_ = f32[32,2,128,128]{3,2,1,0:T(8,128)S(1)} custom-call(f32[128,2,32,128]{3,2,1,0:T(8,128)} %all-to-all-done.refs_0_, bf16[256,256]{1,0:T(8,128)(2,1)S(1)} %get-tuple-element.27.refs_1_, bf16[256,256]{1,0:T(8,128)(2,1)S(1)} %get-tuple-element.26.refs_2_, f32[128,128]{1,0:T(8,128)S(1)} %get-tuple-element.39.refs_3_, ...), custom_call_target="tpu_custom_call" | custom-call | flops 8589934592 | bytes 8388608 | tf_op jit(solution)/shard_map/forward/pallas_call | solution.py:178
  148.1 0.0 copy-done
  148.1 4.0 %inner.1.refs_12_ = f32[2,4,128,8,128]{4,3,2,1,0:T(8,128)} custom-call(s32[16]{0:T(128)S(1)} %add_minimum_fusion.refs_0_, f32[32,2,128,128]{3,2,1,0:T(8,128)S(1)} %forward.1.refs_1_, f32[11,128,128]{2,1,0:T(8,128)S(1)} %fusion.4.refs_2_.refs_4_, f32[32,2,128,128]{3,2,1,0:T(8,128)S(1)} %copy-done, bf16[256,256]{1,0:T(8,128)(2,1)S(1)} %get-tuple-element.15.refs_4_.refs_6_, ...), custom_call_target="tpu_custom_call" | custom-call | flops 3221225472 | bytes 4194304 | tf_op jit(solution)/shard_map/inner/pallas_call | solution.py:266
  152.1 0.0 collective-permute-done.1.refs_3_
  152.1 4.2 %collective-permute-done.refs_2_ = f32[2,1040,128]{2,1,0:T(8,128)S(1)} collective-permute-done((f32[2,1040,128]{2,1,0:T(8,128)S(1)}, f32[2,1040,128]{2,1,0:T(8,128)S(1)}, u32[]{:S(2)}, u32[]{:S(2)}) %collective-permute-start) | collective-permute-done | bytes 1064992 | tf_op jit(solution)/shard_map/ppermute | solution.py:49
  156.4 8.5 %outer.1 = f32[2,4,128,8,128]{4,3,2,1,0:T(8,128)} custom-call(s32[16]{0:T(128)S(1)} %add_minimum_fusion.refs_0_, f32[32,2,128,128]{3,2,1,0:T(8,128)S(1)} %forward.1.refs_1_, f32[2,1040,128]{2,1,0:T(8,128)S(1)} %collective-permute-done.refs_2_, f32[3,2,128,128]{3,2,1,0:T(8,128)S(1)} %collective-permute-done.1.refs_3_, ...), custom_call_target="tpu_custom_call", output_to_operand_aliasing={{}: (12, {})} | custom-call | flops 9663676416 | bytes 12582912 | tf_op jit(solution)/shard_map/outer/pallas_call | solution.py:266
  (9 shorter events, 0.0 us)
Async XLA Ops:
  4.8 27.5 %copy-start.1 = (s32[32]{0:T(128)S(1)}, s32[32]{0:T(128)}, u32[]{:S(2)}) copy-start(s32[32]{0:T(128)} %param.7) | copy-start | bytes 388
  4.8 30.1 %copy-start.4 = (s32[32]{0:T(128)S(1)}, s32[32]{0:T(128)}, u32[]{:S(2)}) copy-start(s32[32]{0:T(128)} %param.8) | copy-start | bytes 388
  4.9 31.6 %copy-start.2 = (s32[16]{0:T(128)S(1)}, s32[16]{0:T(128)}, u32[]{:S(2)}) copy-start(s32[16]{0:T(128)} %constant.247.clone) | copy-start | bytes 196
  4.9 31.6 %copy-start.3 = (s32[16]{0:T(128)S(1)}, s32[16]{0:T(128)}, u32[]{:S(2)}) copy-start(s32[16]{0:T(128)} %constant.246.clone) | copy-start | bytes 196
  4.9 125.4 %all-to-all-start = ((f32[128,2,32,128]{3,2,1,0:T(8,128)}), f32[128,2,32,128]{3,2,1,0:T(8,128)}, u32[]{:S(2)}, u32[]{:S(2)}) async-start(f32[128,2,32,128]{3,2,1,0:T(8,128)} %bitcast.7), calls=%async_computation | async-start | bytes 8388608 | tf_op jit(solution)/shard_map/all_to_all | solution.py:350
  38.8 2.5 %copy-start.5 = (f32[32]{0:T(128)S(1)}, f32[32]{0:T(128)}, u32[]{:S(2)}) copy-start(f32[32]{0:T(128)} %param.9) | copy-start | bytes 388
  135.3 16.8 %collective-permute-start.1 = (f32[3,2,128,128]{3,2,1,0:T(8,128)S(1)}, f32[3,2,128,128]{3,2,1,0:T(8,128)S(1)}, u32[]{:S(2)}, u32[]{:S(2)}) collective-permute-start(f32[3,2,128,128]{3,2,1,0:T(8,128)S(1)} %get-tuple-element.8), channel_id=1, source_target_pairs={{0,1},{1,2},{2,3},{3,4},{4,5},{5,6},{6,7},{7,8},{8,9},{9,10},{10,1... | collective-permute-start | bytes 1179656 | tf_op jit(solution)/shard_map/ppermute | solution.py:49
  138.8 17.5 %collective-permute-start = (f32[2,1040,128]{2,1,0:T(8,128)S(1)}, f32[2,1040,128]{2,1,0:T(8,128)S(1)}, u32[]{:S(2)}, u32[]{:S(2)}) collective-permute-start(f32[2,1040,128]{2,1,0:T(8,128)S(1)} %get-tuple-element.7), channel_id=1, source_target_pairs={{1,0},{2,1},{3,2},{4,3},{5,4},{6,5},{7,6},{8,7},{9,8},{10,9},{11,1... | collective-permute-start | bytes 3194888 | tf_op jit(solution)/shard_map/ppermute | solution.py:49
  140.8 7.4 %copy-start = (f32[32,2,128,128]{3,2,1,0:T(8,128)S(1)}, f32[32,2,128,128]{3,2,1,0:T(8,128)}, u32[]{:S(2)}) copy-start(f32[32,2,128,128]{3,2,1,0:T(8,128)} %pad_maximum_fusion.refs_3_.refs_5_) | copy-start | bytes 12582916

commit v3 on v2

--- a/solution.py
+++ b/solution.py
@@ -105,46 +105,103 @@
     )
 
 
-def halo_body(*refs):
-    x, up_tables, down_tables = refs[0], refs[1:7], refs[7:13]
-    up, down, xs, sems = refs[13:]
+def up_body(*refs):
+    x, tables = refs[0], refs[1:7]
+    up, xs, sems = refs[7:]
     fetch = fetcher(x, xs, sems)
-    for g in (0, 1, 3):
+    for g in (0, 1):
         for part in range(2):
             fetch(g, part).start()
-    for g in (0, 1, 3):
-        for part in range(2):
-            fetch(g, part).wait()
-        for row in range(8 * g, 8 * g + 8, 2):
-            if g < 3:
-                re0, re1, im0, im1 = forward_pair(xs, row, up_tables)
-                for r, re, im in ((row, re0, im0), (row + 1, re1, im1)):
-                    if r < UPPER:
-                        start, size = STARTS[r], 8 * SIDES[r]
-                        for part, value in enumerate((re, im)):
-                            up[part, start : start + size, :] = value[:size]
-                            up[part, start + size : start + 2 * size, :] = value[FACTOR - size :]
-            elif row + 1 >= 32 - LOWER:
-                re0, re1, im0, im1 = forward_pair(xs, row, down_tables)
-                for r, re, im in ((row, re0, im0), (row + 1, re1, im1)):
-                    if r >= 32 - LOWER:
-                        down[r - 32 + LOWER, 0] = re
-                        down[r - 32 + LOWER, 1] = im
-
-
-def halo(x, up_tables, down_tables):
+    for row in range(0, UPPER, 2):
+        if row % 8 == 0:
+            for part in range(2):
+                fetch(row // 8, part).wait()
+        re0, re1, im0, im1 = forward_pair(xs, row, tables)
+        for r, re, im in ((row, re0, im0), (row + 1, re1, im1)):
+            if r < UPPER:
+                start, size = STARTS[r], 8 * SIDES[r]
+                for part, value in enumerate((re, im)):
+                    up[part, start : start + size, :] = value[:size]
+                    up[part, start + size : start + 2 * size, :] = value[FACTOR - size :]
+
+
+def down_body(*refs):
+    x, tables = refs[0], refs[1:7]
+    _, down, xs, sems = refs[7:]
+    fetch = fetcher(x, xs, sems)
+    for part in range(2):
+        fetch(3, part).start()
+    for part in range(2):
+        fetch(3, part).wait()
+    for row in (28, 30):
+        re0, re1, im0, im1 = forward_pair(xs, row, tables)
+        for r, re, im in ((row, re0, im0), (row + 1, re1, im1)):
+            if r >= 32 - LOWER:
+                down[r - 32 + LOWER, 0] = re
+                down[r - 32 + LOWER, 1] = im
+
+
+def halo(body, shape, pairs, name, x, tables, after=None):
+    first = [] if after is None else [after]
     return pl.pallas_call(
-        halo_body,
-        in_specs=[pl.BlockSpec(memory_space=pl.ANY)] + [pl.BlockSpec(memory_space=pltpu.VMEM)] * 12,
-        out_shape=[
-            jax.ShapeDtypeStruct((2, STARTS[-1], FACTOR), jnp.float32),
-            jax.ShapeDtypeStruct((LOWER, 2) + PLANE, jnp.float32),
-        ],
+        body,
+        in_specs=[pl.BlockSpec(memory_space=pl.ANY)]
+        + [pl.BlockSpec(memory_space=pltpu.VMEM)] * 6
+        + [pl.BlockSpec(memory_space=pl.ANY)] * len(first),
+        out_shape=jax.ShapeDtypeStruct(shape, jnp.float32),
         scratch_shapes=[pltpu.VMEM((FACTOR * PITCH, FACTOR), jnp.float32), pltpu.SemaphoreType.DMA((4, 2))],
         compiler_params=pltpu.CompilerParams(vmem_limit_bytes=16 << 20),
-        cost_estimate=pl.CostEstimate(flops=5 << 30, bytes_accessed=5 << 20, transcendentals=0),
-        name="halo",
-    )(x, *up_tables, *down_tables)
+        cost_estimate=pl.CostEstimate(flops=pairs << 29, bytes_accessed=pairs << 19, transcendentals=0),
+        name=name,
+    )(x, *tables, *first)
+
+
+def up_rows(x, tables):
+    return halo(up_body, (2, STARTS[-1], FACTOR), 8, "up", x, tables)
+
+
+def down_rows(x, tables, after):
+    return halo(down_body, (LOWER, 2) + PLANE, 2, "down", x, tables, after)
+
+
+def arrange_body(x, out, stage, sems):
+    parts, spans = x.shape[0], sems.shape[1]
+    share = x.shape[1] // spans
+
+    def take(i, part):
+        span = pl.ds(i * share, share)
+        return pltpu.make_async_copy(x.at[part, span], stage.at[span, part], sems.at[part, i])
+
+    def give(i):
+        span = pl.ds(i * share, share)
+        return pltpu.make_async_copy(stage.at[span], out.at[span], sems.at[parts, i])
+
+    for i in range(spans):
+        for part in range(parts):
+            take(i, part).start()
+    for i in range(spans):
+        for part in range(parts):
+            take(i, part).wait()
+        give(i).start()
+    for i in range(spans):
+        give(i).wait()
+
+
+def arrange(blocks):
+    parts, devices, rows, width = blocks.shape
+    return pl.pallas_call(
+        arrange_body,
+        in_specs=[pl.BlockSpec(memory_space=pl.ANY)],
+        out_specs=pl.BlockSpec(memory_space=pl.ANY),
+        out_shape=jax.ShapeDtypeStruct((devices, parts, rows, width), jnp.float32),
+        scratch_shapes=[
+            pltpu.VMEM((devices, parts, rows, width), jnp.float32),
+            pltpu.SemaphoreType.DMA((parts + 1, 8)),
+        ],
+        compiler_params=pltpu.CompilerParams(vmem_limit_bytes=60 << 20),
+        cost_estimate=pl.CostEstimate(flops=1 << 20, bytes_accessed=8 << 20, transcendentals=0),
+        name="arrange",
+    )(blocks)
 
 
 def forward_body(*refs):
@@ -216,29 +273,36 @@
 
 
 def inner_body(*refs):
-    taps, spec, weights, chirp = refs[:4]
-    tables, (out, ext, sems) = refs[4:10], refs[10:]
-    first, count = 8 - LOWER, 8 + LOWER + UPPER
-    copy = pltpu.make_async_copy(spec.at[pl.ds(first, count)], ext.at[pl.ds(8, count)], sems.at[0])
-    copy.start()
-    copy.wait()
-    view = out.reshape(2 * FACTOR * 8, FACTOR)
-    for local in (0, 4):
-        focus_rows(ext, taps, weights, chirp, tables, view, 8, local)
-
-
-def outer_body(*refs):
-    taps, spec, up, down, weights, chirp = refs[:6]
-    tables, (_, out, ext, sems) = refs[6:12], refs[12:]
+    taps, spec, down, weights, chirp = refs[:5]
+    tables, (out, ext, sems) = refs[5:11], refs[11:]
     step = pl.program_id(0)
-    rows = spec.shape[0]
+    count = 16 + UPPER
 
     @pl.when(step == 0)
     def _():
-        copy = pltpu.make_async_copy(spec, ext.at[pl.ds(LOWER, rows)], sems.at[0])
+        copy = pltpu.make_async_copy(spec.at[pl.ds(0, count)], ext.at[pl.ds(LOWER, count)], sems.at[0])
         copy.start()
         for r in range(LOWER):
             ext[r] = down[r]
+        copy.wait()
+
+    view = out.reshape(2 * FACTOR * 8, FACTOR)
+    for local in (0, 4):
+        focus_rows(ext, taps, weights, chirp, tables, view, 8 * step, local)
+
+
+def outer_body(*refs):
+    taps, spec, up, weights, chirp = refs[:5]
+    tables, (_, out, ext, sems) = refs[5:11], refs[11:]
+    step = pl.program_id(0)
+    rows = spec.shape[0]
+    first = rows // 2 - LOWER
+
+    @pl.when(step == 0)
+    def _():
+        count = rows - first
+        copy = pltpu.make_async_copy(spec.at[pl.ds(first, count)], ext.at[pl.ds(first + LOWER, count)], sems.at[0])
+        copy.start()
         for r in range(UPPER):
             start, size = STARTS[r], 8 * SIDES[r]
             for part in range(2):
@@ -247,9 +311,8 @@
         copy.wait()
 
     view = out.reshape(2 * FACTOR * 8, FACTOR)
-    base = 8 * (step + jnp.minimum(step, 1))
     for local in (0, 4):
-        focus_rows(ext, taps, weights, chirp, tables, view, base, local)
+        focus_rows(ext, taps, weights, chirp, tables, view, rows // 2 + 8 * step, local)
 
 
 def focus(group_of, steps, body, taps, operands, kinds, weights, chirp, tables, rows, prior, name):
@@ -332,22 +395,23 @@
     rows = received.shape[2]
     taps, weights, chirp = spectral_tables(distance, chirp_rate)
     inverse = transform_tables(own, 1)
-    up, down = halo(received, transform_tables(below, -1), transform_tables(above, -1))
+    up = up_rows(received, transform_tables(below, -1))
+    down = down_rows(received, transform_tables(above, -1), up)
     up, down = exchange(up, down)
     spec = forward(received, transform_tables(own, -1))
     anywhere = pl.BlockSpec(memory_space=pl.ANY)
-    image = focus(lambda g: 1, 1, inner_body, taps, [spec], [anywhere], weights, chirp, inverse, rows, None, "inner")
-    kinds = [anywhere, whole(up.shape), whole(down.shape)]
-    later = lambda g: g + jnp.minimum(g, 1)
-    image = focus(later, 3, outer_body, taps, [spec, up, down], kinds, weights, chirp, inverse, rows, image, "outer")
+    half = rows // 16
+    shared = (weights, chirp, inverse, rows)
+    image = focus(lambda g: g, half, inner_body, taps, [spec, down], [anywhere, whole(down.shape)], *shared, None, "inner")
+    image = focus(lambda g: g + half, half, outer_body, taps, [spec, up], [anywhere, whole(up.shape)], *shared, image, "outer")
     return image.transpose(0, 1, 3, 2, 4).reshape(2, rows, PULSES)
 
 
 def per_device(raw_echo, centroid, shifts, chirp_rate):
     devices = lax.axis_size("row")
     own_rows = raw_echo.shape[1] // devices
-    blocks = raw_echo.reshape(2, devices, own_rows, raw_echo.shape[2]).transpose(1, 0, 2, 3)
-    received = lax.all_to_all(blocks, "row", split_axis=0, concat_axis=0, tiled=True)
+    blocks = raw_echo.reshape(2, devices, own_rows, raw_echo.shape[2])
+    received = lax.all_to_all(arrange(blocks), "row", split_axis=0, concat_axis=0, tiled=True)
 
     def pick(values, device):
         block = jnp.clip(device, 0, devices - 1) * own_rows // BLOCK

time: 165 us -> 163 us (0.988)
  Pallas kernels: 24.9 us -> 30.2 us
  local copies, waits for them, and re-layouts: 5.03 us -> 0.2 us
  waiting for transfers between devices: 79.8 us -> 75.4 us
    pallas_call x1 -> x3, Pallas kernels: 5.04 us -> 9.96 us  [the longest x2 6.31 us: halo(): pl.pallas_call(body, in_specs=[pl.BlockSpec(memory_space=pl.ANY)] + [pl.B...]
    reshape x1 -> x0, local copies, waits for them, and re-layouts: 4.85 us -> none  [per_device(): raw_echo.reshape(2, devices, own_rows, raw_echo.shape[2])]
    ppermute x2, waiting for transfers between devices: 4.24 us -> 0.01 us  [from_behind(): return lax.ppermute(shard, axis, pairs)]
  transfers between devices with their start and end apart: 3 -> 3, of which waited for: 2 -> 1; matrix products, arithmetic and copies ran while one was open for 12% -> 12% of each run, Pallas kernels for 7% -> 10%
where the time goes in v3:
time: 163 us
  waiting for transfers between devices  75.4 us (46%)
  starting transfers between devices  34.3 us (21%)
  Pallas kernels  30.2 us (19%)
  other arithmetic  19.3 us (12%)
  between operations  3.4 us (2%)
    all_to_all x1, waiting for transfers between devices, per_device(): lax.all_to_all(arrange(blocks), 'row', split_axis=0, concat_axis=0, tiled...  75.3 us
    all_to_all x1, starting transfers between devices, per_device(): lax.all_to_all(arrange(blocks), 'row', split_axis=0, concat_axis=0, tiled...  27.5 us
    pallas_call x2, Pallas kernels, focus(): pl.pallas_call(body, grid=(steps,), in_specs=specs, out_specs=image, out_...  12.9 us
    mul x1, other arithmetic, spectral_tables(): window * jnp.cos(phase)  7.68 us
    pallas_call x1, Pallas kernels, forward(): pl.pallas_call(forward_body, grid=(rows // 8,), in_specs=[pl.BlockSpec(me...  7.33 us
    ppermute x2, starting transfers between devices, from_behind(): return lax.ppermute(shard, axis, pairs)  6.83 us
    pallas_call x2, Pallas kernels, halo(): pl.pallas_call(body, in_specs=[pl.BlockSpec(memory_space=pl.ANY)] + [pl.B...  6.31 us
    pallas_call x1, Pallas kernels, arrange(): pl.pallas_call(arrange_body, in_specs=[pl.BlockSpec(memory_space=pl.ANY)]...  3.65 us
  transfers between devices with their start and end apart: 3, of which 1 were waited for; matrix products, arithmetic and copies ran while one was open for 12% of the time, Pallas kernels for 10%

profile of v3, /device:TPU:519, one launch (start us, length us, event | category | flops | bytes accessed | tf_op | source)
XLA Modules:
  0.0 162.8 jit_solution(1150753320991894301)
XLA Ops:
  0.0 3.7 %arrange.1 = f32[128,2,32,128]{3,2,1,0:T(8,128)} custom-call(f32[2,128,32,128]{3,2,1,0:T(8,128)} %bitcast.4), custom_call_target="tpu_custom_call" | custom-call | flops 1048576 | bytes 8388608 | tf_op jit(solution)/shard_map/arrange/pallas_call | solution.py:192
  3.7 0.0 copy-start.1
  3.7 0.0 copy-start.4
  3.7 0.0 copy-start.2
  3.7 0.0 copy-start.3
  3.7 27.5 %all-to-all-start = ((f32[128,2,32,128]{3,2,1,0:T(8,128)}), f32[128,2,32,128]{3,2,1,0:T(8,128)}, u32[]{:S(2)}, u32[]{:S(2)}) async-start(f32[128,2,32,128]{3,2,1,0:T(8,128)} %arrange.1), calls=%async_computation | async-start | bytes 8388608 | tf_op jit(solution)/shard_map/all_to_all | solution.py:414
  31.2 0.0 copy-done.1
  31.2 0.7 fusion.120
  34.0 0.0 copy-done.4
  34.0 0.7 fusion.117
  35.5 0.0 copy-done.2
  35.5 0.0 copy-done.3
  35.5 0.7 add_minimum_fusion.refs_0_
  36.2 0.1 broadcast_in_dim.23
  36.3 0.1 add.296
  36.5 0.3 fusion.92
  36.8 0.6 fusion.94
  37.4 0.1 fusion.18
  37.5 0.3 fusion.104
  37.9 0.0 copy-start.5
  37.9 0.6 fusion.106
  38.5 0.1 fusion.14
  38.5 0.6 broadcast_multiply_fusion.3
  39.1 1.0 broadcast_multiply_fusion.2
  40.1 0.1 fusion.16
  40.2 0.1 fusion.12
  40.3 0.0 copy-done.5
  40.3 0.5 add_multiply_fusion
  40.9 7.7 %fusion = (f32[32,1,128,128]{3,2,1,0:T(8,128)S(1)}, f32[32,1,128,128]{3,2,1,0:T(8,128)S(1)}) fusion(f32[128,128]{1,0:T(8,128)S(1)} %get-tuple-element.53, f32[32]{0:T(128)S(1)} %broadcast_multiply_fusion.8, f32[128,128]{1,0:T(8,128)S(1)} %get-tuple-element.50), kind=kLoop, calls=%fused_computation.3 | loop fusion | flops 1572864 | bytes 4325504 | tf_op jit(solution)/shard_map/mul | solution.py:391
  48.5 2.2 %pad_maximum_fusion.refs_4_ = f32[32,2,128,128]{3,2,1,0:T(8,128)} fusion(f32[32,1,128,128]{3,2,1,0:T(8,128)S(1)} %get-tuple-element.25, f32[32,1,128,128]{3,2,1,0:T(8,128)S(1)} %get-tuple-element.24), kind=kLoop, calls=%fused_computation | loop fusion | flops 1048576 | bytes 8388608 | tf_op jit(solution)/shard_map/stack | solution.py:391
  50.8 3.0 %fusion.4.refs_3_ = f32[11,128,128]{2,1,0:T(8,128)S(1)} fusion(f32[128,128]{1,0:T(8,128)S(1)} %get-tuple-element.52, s32[11,128]{1,0:T(8,128)S(1)} %get-tuple-element.56, s32[128,128]{1,0:T(8,128)S(1)} %get-tuple-element.51, f32[128,128]{1,0:T(8,128)S(1)} %get-tuple-element.54, f32[11,128]{1,0:T(8,128)S(1)} %get-tuple-element.55), kind=kLoop, calls=%fused_computation.16 | loop fusion | flops 4866048 | bytes 928768 | tf_op jit(solution)/shard_map/jit(_where)/select_n | solution.py:388
  53.8 75.3 %all-to-all-done.refs_0_ = f32[128,2,32,128]{3,2,1,0:T(8,128)} async-done(((f32[128,2,32,128]{3,2,1,0:T(8,128)}), f32[128,2,32,128]{3,2,1,0:T(8,128)}, u32[]{:S(2)}, u32[]{:S(2)}) %all-to-all-start) | async-done | bytes 4194336 | tf_op jit(solution)/shard_map/all_to_all | solution.py:414
  129.1 4.1 %up.1.refs_7_ = f32[2,1040,128]{2,1,0:T(8,128)S(1)} custom-call(f32[128,2,32,128]{3,2,1,0:T(8,128)} %all-to-all-done.refs_0_, bf16[256,256]{1,0:T(8,128)(2,1)S(1)} %get-tuple-element.19.refs_1_, bf16[256,256]{1,0:T(8,128)(2,1)S(1)} %get-tuple-element.18.refs_2_, f32[128,128]{1,0:T(8,128)S(1)} %get-tuple-element.64.refs_3_, ...), custom_call_target="tpu_custom_call" | custom-call | flops 4294967296 | bytes 4194304 | tf_op jit(solution)/shard_map/up/pallas_call | solution.py:146
  133.2 3.2 %collective-permute-start = (f32[2,1040,128]{2,1,0:T(8,128)S(1)}, f32[2,1040,128]{2,1,0:T(8,128)S(1)}, u32[]{:S(2)}, u32[]{:S(2)}) collective-permute-start(f32[2,1040,128]{2,1,0:T(8,128)S(1)} %up.1.refs_7_), channel_id=1, source_target_pairs={{1,0},{2,1},{3,2},{4,3},{5,4},{6,5},{7,6},{8,7},{9,8},{10,9},{11,1... | collective-permute-start | bytes 3194888 | tf_op jit(solution)/shard_map/ppermute | solution.py:49
  136.4 2.2 %down.1 = f32[3,2,128,128]{3,2,1,0:T(8,128)S(1)} custom-call(f32[128,2,32,128]{3,2,1,0:T(8,128)} %all-to-all-done.refs_0_, bf16[256,256]{1,0:T(8,128)(2,1)S(1)} %get-tuple-element.11.refs_1_, bf16[256,256]{1,0:T(8,128)(2,1)S(1)} %get-tuple-element.10.refs_2_, f32[128,128]{1,0:T(8,128)S(1)} %get-tuple-element.33.refs_3_, ...), custom_call_target="tpu_custom_call" | custom-call | flops 1073741824 | bytes 1048576 | tf_op jit(solution)/shard_map/down/pallas_call | solution.py:146
  138.7 3.6 %collective-permute-start.1 = (f32[3,2,128,128]{3,2,1,0:T(8,128)S(1)}, f32[3,2,128,128]{3,2,1,0:T(8,128)S(1)}, u32[]{:S(2)}, u32[]{:S(2)}) collective-permute-start(f32[3,2,128,128]{3,2,1,0:T(8,128)S(1)} %down.1), channel_id=1, source_target_pairs={{0,1},{1,2},{2,3},{3,4},{4,5},{5,6},{6,7},{7,8},{8,9},{9,10},{10,1... | collective-permute-start | bytes 1179656 | tf_op jit(solution)/shard_map/ppermute | solution.py:49
  142.3 0.0 copy-start
  142.3 7.3 %forward.1.refs_1_ = f32[32,2,128,128]{3,2,1,0:T(8,128)S(1)} custom-call(f32[128,2,32,128]{3,2,1,0:T(8,128)} %all-to-all-done.refs_0_, bf16[256,256]{1,0:T(8,128)(2,1)S(1)} %get-tuple-element.23.refs_1_, bf16[256,256]{1,0:T(8,128)(2,1)S(1)} %get-tuple-element.22.refs_2_, f32[128,128]{1,0:T(8,128)S(1)} %get-tuple-element.43.refs_3_, ...), custom_call_target="tpu_custom_call" | custom-call | flops 8589934592 | bytes 8388608 | tf_op jit(solution)/shard_map/forward/pallas_call | solution.py:235
  149.7 0.0 collective-permute-done.1.refs_2_
  149.7 0.0 copy-done
  149.7 6.5 %inner.1.refs_11_ = f32[2,4,128,8,128]{4,3,2,1,0:T(8,128)} custom-call(s32[16]{0:T(128)S(1)} %add_minimum_fusion.refs_0_, f32[32,2,128,128]{3,2,1,0:T(8,128)S(1)} %forward.1.refs_1_, f32[3,2,128,128]{3,2,1,0:T(8,128)S(1)} %collective-permute-done.1.refs_2_, f32[11,128,128]{2,1,0:T(8,128)S(1)} %fusion.4.refs_3_, f32[32,2,128,128]{3,2,1,0:T(8,128)S(1)} %copy-done, ...), custom_call_target="tpu_custom_call" | custom-call | flops 6442450944 | bytes 8388608 | tf_op jit(solution)/shard_map/inner/pallas_call | solution.py:329
  156.2 0.0 collective-permute-done.refs_2_
  156.2 6.4 %outer.1 = f32[2,4,128,8,128]{4,3,2,1,0:T(8,128)} custom-call(s32[16]{0:T(128)S(1)} %add_minimum_fusion.refs_0_, f32[32,2,128,128]{3,2,1,0:T(8,128)S(1)} %forward.1.refs_1_, f32[2,1040,128]{2,1,0:T(8,128)S(1)} %collective-permute-done.refs_2_, f32[11,128,128]{2,1,0:T(8,128)S(1)} %fusion.4.refs_3_, ...), custom_call_target="tpu_custom_call", output_to_operand_aliasing={{}: (11, {})} | custom-call | flops 6442450944 | bytes 8388608 | tf_op jit(solution)/shard_map/outer/pallas_call | solution.py:329
  (9 shorter events, 0.0 us)
Async XLA Ops:
  3.7 27.6 %copy-start.1 = (s32[32]{0:T(128)S(1)}, s32[32]{0:T(128)}, u32[]{:S(2)}) copy-start(s32[32]{0:T(128)} %param.7) | copy-start | bytes 388
  3.7 30.3 %copy-start.4 = (s32[32]{0:T(128)S(1)}, s32[32]{0:T(128)}, u32[]{:S(2)}) copy-start(s32[32]{0:T(128)} %param.8) | copy-start | bytes 388
  3.7 31.8 %copy-start.2 = (s32[16]{0:T(128)S(1)}, s32[16]{0:T(128)}, u32[]{:S(2)}) copy-start(s32[16]{0:T(128)} %constant.247.clone) | copy-start | bytes 196
  3.7 31.8 %copy-start.3 = (s32[16]{0:T(128)S(1)}, s32[16]{0:T(128)}, u32[]{:S(2)}) copy-start(s32[16]{0:T(128)} %constant.246.clone) | copy-start | bytes 196
  3.7 125.4 %all-to-all-start = ((f32[128,2,32,128]{3,2,1,0:T(8,128)}), f32[128,2,32,128]{3,2,1,0:T(8,128)}, u32[]{:S(2)}, u32[]{:S(2)}) async-start(f32[128,2,32,128]{3,2,1,0:T(8,128)} %arrange.1), calls=%async_computation | async-start | bytes 8388608 | tf_op jit(solution)/shard_map/all_to_all | solution.py:414
  37.9 2.5 %copy-start.5 = (f32[32]{0:T(128)S(1)}, f32[32]{0:T(128)}, u32[]{:S(2)}) copy-start(f32[32]{0:T(128)} %param.9) | copy-start | bytes 388
  133.2 22.9 %collective-permute-start = (f32[2,1040,128]{2,1,0:T(8,128)S(1)}, f32[2,1040,128]{2,1,0:T(8,128)S(1)}, u32[]{:S(2)}, u32[]{:S(2)}) collective-permute-start(f32[2,1040,128]{2,1,0:T(8,128)S(1)} %up.1.refs_7_), channel_id=1, source_target_pairs={{1,0},{2,1},{3,2},{4,3},{5,4},{6,5},{7,6},{8,7},{9,8},{10,9},{11,1... | collective-permute-start | bytes 3194888 | tf_op jit(solution)/shard_map/ppermute | solution.py:49
  138.7 11.0 %collective-permute-start.1 = (f32[3,2,128,128]{3,2,1,0:T(8,128)S(1)}, f32[3,2,128,128]{3,2,1,0:T(8,128)S(1)}, u32[]{:S(2)}, u32[]{:S(2)}) collective-permute-start(f32[3,2,128,128]{3,2,1,0:T(8,128)S(1)} %down.1), channel_id=1, source_target_pairs={{0,1},{1,2},{2,3},{3,4},{4,5},{5,6},{6,7},{7,8},{8,9},{9,10},{10,1... | collective-permute-start | bytes 1179656 | tf_op jit(solution)/shard_map/ppermute | solution.py:49
  142.3 7.4 %copy-start = (f32[32,2,128,128]{3,2,1,0:T(8,128)S(1)}, f32[32,2,128,128]{3,2,1,0:T(8,128)}, u32[]{:S(2)}) copy-start(f32[32,2,128,128]{3,2,1,0:T(8,128)} %pad_maximum_fusion.refs_4_) | copy-start | bytes 12582916

commit v4 on v3

v4 whole, which is shorter than its diff:
```python
import math

import jax
import jax.numpy as jnp
from jax import lax
from jax.experimental import pallas as pl
from jax.experimental.pallas import tpu as pltpu
from jax.sharding import PartitionSpec as P

FACTOR = 128
PULSES = 16384
BLOCK = 128
MAXSHIFT = 12
TAPS = 4
LOWER = TAPS - 1
UPPER = MAXSHIFT + TAPS - 1
PITCH = 72
TILES = FACTOR // 8
PLANE = (FACTOR, FACTOR)
DEPTH = FACTOR + 8
PADDED = (DEPTH, FACTOR)
TABLE = (2 * FACTOR, 2 * FACTOR)


def edge(tile):
    return min(tile, TILES - 1 - tile)


def last_tap(tile):
    return math.ceil(4 * MAXSHIFT * ((8 - edge(tile)) / TILES) ** 2) + TAPS - 1


def tap_count(tile):
    near, far = (7 - edge(tile)) / TILES, (8 - edge(tile)) / TILES
    return max(math.ceil(4 * s * far**2) - math.floor(4 * s * near**2) + 2 * TAPS - 1 for s in range(MAXSHIFT + 1))


def side_tiles(row):
    return sum(4 * MAXSHIFT * ((8 - e) / TILES) ** 2 > row - LOWER for e in range(TILES // 2))


COUNTS = [tap_count(t) for t in range(TILES)]
LASTS = [last_tap(t) for t in range(TILES)]
SIDES = [side_tiles(j) for j in range(UPPER)]
STARTS = [16 * sum(SIDES[:j]) for j in range(UPPER + 1)]


def from_behind(shard, axis, by):
    devices = lax.axis_size(axis)
    pairs = [(i, i + by) for i in range(devices) if 0 <= i + by < devices]
    return lax.ppermute(shard, axis, pairs)


def split(values):
    high = values.astype(jnp.bfloat16)
    low = (values - high.astype(jnp.float32)).astype(jnp.bfloat16)
    return high, low


def stack2(a, b, c, d):
    return jnp.concatenate([jnp.concatenate([a, b], axis=1), jnp.concatenate([c, d], axis=1)], axis=0)


def multiply(table, data, across):
    dims = (((1,), (1 if across else 0,)), ((), ()))

    def dot(x, y):
        return lax.dot_general(x, y, dims, preferred_element_type=jnp.float32)

    high, low = split(data)
    half = 2 * FACTOR
    both = dot(table[...], high)
    return both[:half] + dot(table[:half, :], low) + both[half:]


def quarters(values):
    n = FACTOR
    return values[:n, :n], values[:n, n:], values[n:, :n], values[n:, n:]


def transform_pairs(pairs, first, twist, second, sign):
    middle = [multiply(first, stack2(*pair), False) for pair in pairs]
    c, s = twist[0][...], twist[1][...]
    turned = []
    for a in middle:
        r0, r1, i0, i1 = quarters(a)
        if sign < 0:
            turned.append(stack2(r0 * c + i0 * s, i0 * c - r0 * s, r1 * c + i1 * s, i1 * c - r1 * s))
        else:
            turned.append(stack2(r0 * c - i0 * s, i0 * c + r0 * s, r1 * c - i1 * s, i1 * c + r1 * s))
    return [quarters(multiply(second, t, True)) for t in turned]


def fetcher(x, xs, sems):
    view = xs.reshape(FACTOR, PITCH, FACTOR)

    def fetch(g, part):
        rows = pl.ds(pl.multiple_of(8 * g, 8), 8)
        target = pl.ds(pl.multiple_of(32 * part + 8 * g, 8), 8)
        return pltpu.make_async_copy(x.at[:, part, rows, :], view.at[:, target, :], sems.at[g, part])

    return fetch


def forward_rows(xs, rows, tables):
    def load(part, r):
        return xs[pl.ds(32 * part + r, FACTOR, stride=PITCH), :]

    pairs = [(load(0, row), load(0, row + 1), load(1, row), load(1, row + 1)) for row in rows]
    results = transform_pairs(pairs, tables[0], tables[1:3], tables[3], -1)
    for row, (re0, re1, im0, im1) in zip(rows, results):
        yield row, re0, im0
        yield row + 1, re1, im1


def halo_body(*refs):
    x, up_tables, down_tables = refs[0], refs[1:5], refs[5:9]
    up, down, xs, sems = refs[9:]
    fetch = fetcher(x, xs, sems)
    for g in (0, 1, 3):
        for part in range(2):
            fetch(g, part).start()
    for first in range(0, UPPER, 4):
        if first % 8 == 0:
            for part in range(2):
                fetch(first // 8, part).wait()
        for r, re, im in forward_rows(xs, (first, first + 2), up_tables):
            if r < UPPER:
                start, size = STARTS[r], 8 * SIDES[r]
                for part, value in enumerate((re, im)):
                    up[part, start : start + size, :] = value[:size]
                    up[part, start + size : start + 2 * size, :] = value[FACTOR - size :]
    for part in range(2):
        fetch(3, part).wait()
    for r, re, im in forward_rows(xs, (28, 30), down_tables):
        if r >= 32 - LOWER:
            down[r - 32 + LOWER, 0] = re
            down[r - 32 + LOWER, 1] = im


def halo(x, up_tables, down_tables):
    shapes = [(2, STARTS[-1], FACTOR), (LOWER, 2) + PLANE]
    return pl.pallas_call(
        halo_body,
        in_specs=[pl.BlockSpec(memory_space=pl.ANY)] + [pl.BlockSpec(memory_space=pltpu.VMEM)] * 8,
        out_shape=[jax.ShapeDtypeStruct(shape, jnp.float32) for shape in shapes],
        scratch_shapes=[pltpu.VMEM((FACTOR * PITCH, FACTOR), jnp.float32), pltpu.SemaphoreType.DMA((4, 2))],
        compiler_params=pltpu.CompilerParams(vmem_limit_bytes=16 << 20),
        cost_estimate=pl.CostEstimate(flops=5 << 30, bytes_accessed=5 << 20, transcendentals=0),
        name="halo",
    )(x, *up_tables, *down_tables)


def arrange_body(x, out, stage, sems):
    parts, spans = x.shape[0], sems.shape[1]
    share = x.shape[1] // spans

    def take(i, part):
        span = pl.ds(i * share, share)
        return pltpu.make_async_copy(x.at[part, span], stage.at[span, part], sems.at[part, i])

    def give(i):
        span = pl.ds(i * share, share)
        return pltpu.make_async_copy(stage.at[span], out.at[span], sems.at[parts, i])

    for i in range(spans):
        for part in range(parts):
            take(i, part).start()
    for i in range(spans):
        for part in range(parts):
            take(i, part).wait()
        give(i).start()
    for i in range(spans):
        give(i).wait()


def arrange(blocks):
    parts, devices, rows, width = blocks.shape
    return pl.pallas_call(
        arrange_body,
        in_specs=[pl.BlockSpec(memory_space=pl.ANY)],
        out_specs=pl.BlockSpec(memory_space=pl.ANY),
        out_shape=jax.ShapeDtypeStruct((devices, parts, rows, width), jnp.float32),
        scratch_shapes=[
            pltpu.VMEM((devices, parts, rows, width), jnp.float32),
            pltpu.SemaphoreType.DMA((parts + 1, 8)),
        ],
        compiler_params=pltpu.CompilerParams(vmem_limit_bytes=60 << 20),
        cost_estimate=pl.CostEstimate(flops=1 << 20, bytes_accessed=8 << 20, transcendentals=0),
        name="arrange",
    )(blocks)


def forward_body(*refs):
    x, tables = refs[0], refs[1:5]
    spec, xs, sems = refs[5:]
    group = pl.program_id(0)
    fetch = fetcher(x, xs, sems)

    @pl.when(group == 0)
    def _():
        for g in range(4):
            for part in range(2):
                fetch(g, part).start()

    for part in range(2):
        fetch(group, part).wait()
    for local in (0, 4):
        rows = (8 * group + local, 8 * group + local + 2)
        for i, (_, re, im) in enumerate(forward_rows(xs, rows, tables)):
            spec[local + i, 0, :FACTOR, :] = re
            spec[local + i, 1, :FACTOR, :] = im


def whole(shape):
    return pl.BlockSpec(shape, lambda *_: (0,) * len(shape))


def forward(x, tables):
    rows = x.shape[2]
    return pl.pallas_call(
        forward_body,
        grid=(rows // 8,),
        in_specs=[pl.BlockSpec(memory_space=pl.ANY)] + [whole(t.shape) for t in tables],
        out_specs=pl.BlockSpec((8, 2) + PADDED, lambda g: (g, 0, 0, 0)),
        out_shape=jax.ShapeDtypeStruct((rows, 2) + PADDED, jnp.float32),
        scratch_shapes=[pltpu.VMEM((FACTOR * PITCH, FACTOR), jnp.float32), pltpu.SemaphoreType.DMA((4, 2))],
        compiler_params=pltpu.CompilerParams(vmem_limit_bytes=16 << 20),
        cost_estimate=pl.CostEstimate(flops=8 << 30, bytes_accessed=8 << 20, transcendentals=0),
        name="forward",
    )(x, *tables)


def focus_rows(source, shift, taps, weights, chirp, tables, view, first, slot):
    tiles = [[[], []] for _ in range(4)]
    for t in range(TILES):
        sub = slice(8 * t, 8 * t + 8)
        start = first + taps[t] + shift
        w = [weights[k, sub, :] for k in range(COUNTS[t])]
        sums = [[None, None] for _ in range(4)]
        for j in range(COUNTS[t] + 3):
            values = [source[start + j, part, sub, :] for part in range(2)]
            for i in range(4):
                if 0 <= j - i < COUNTS[t]:
                    for part in range(2):
                        term = w[j - i] * values[part]
                        sums[i][part] = term if sums[i][part] is None else sums[i][part] + term
        for i in range(4):
            re, im = sums[i]
            c, s = chirp[first + i, 0, sub, :], chirp[first + i, 1, sub, :]
            tiles[i][0].append(re * c + im * s)
            tiles[i][1].append(im * c - re * s)
    planes = [[jnp.concatenate(part, axis=0) for part in row] for row in tiles]
    pairs = [(planes[i][0], planes[i + 1][0], planes[i][1], planes[i + 1][1]) for i in (0, 2)]
    results = transform_pairs(pairs, tables[0], tables[1:3], tables[3], 1)
    for i, (re0, re1, im0, im1) in zip((0, 2), results):
        for part, r, value in ((0, 0, re0), (0, 1, re1), (1, 0, im0), (1, 1, im1)):
            view[pl.ds(FACTOR * 8 * part + slot + i + r, FACTOR, stride=8), :] = value


GROUP = 2 * FACTOR * 8


def inner_body(*refs):
    taps, spec, down, weights, chirp = refs[:5]
    tables, (out, ext, image, sems) = refs[5:9], refs[9:]
    count = 4 + UPPER
    copy = pltpu.make_async_copy(spec.at[pl.ds(0, count)], ext.at[pl.ds(LOWER, count)], sems.at[0])
    copy.start()
    view = image.reshape(2 * GROUP, FACTOR)
    gives = [pltpu.make_async_copy(image.at[g], out.at[:, g], sems.at[1 + g]) for g in range(2)]

    def quad(k, carry):
        slot = (k // 2) * GROUP + 4 * (k % 2)
        focus_rows(spec, 0, taps, weights, chirp, tables, view, 4 * k, slot)
        return carry

    quad(2, 0)
    quad(3, 0)
    gives[1].start()
    for r in range(LOWER):
        ext[r, :, :FACTOR, :] = down[r]
    copy.wait()
    quad(1, 0)
    focus_rows(ext, LOWER, taps, weights, chirp, tables, view, 0, 0)
    gives[0].start()
    for give in gives:
        give.wait()


def outer_body(*refs):
    taps, spec, up, weights, chirp = refs[:5]
    tables, (_, out, ext, image, sems) = refs[5:9], refs[9:]
    rows = spec.shape[0]
    half = rows // 2
    below = half - LOWER
    copy = pltpu.make_async_copy(spec.at[pl.ds(below, rows - below)], ext.at[pl.ds(0, rows - below)], sems.at[0])
    copy.start()
    for r in range(UPPER):
        start, size = STARTS[r], 8 * SIDES[r]
        for part in range(2):
            ext[rows - below + r, part, :size, :] = up[part, start : start + size, :]
            ext[rows - below + r, part, FACTOR - size : FACTOR, :] = up[part, start + size : start + 2 * size, :]
    copy.wait()
    view = image.reshape(2 * GROUP, FACTOR)

    def give(g):
        return pltpu.make_async_copy(image.at[g], out.at[:, half // 8 + g], sems.at[1 + g])

    def group(g, carry):
        for local in (0, 4):
            focus_rows(ext, -below, taps, weights, chirp, tables, view, half + 8 * g + local, GROUP * g + local)
        give(g).start()
        return carry

    lax.fori_loop(0, 2, group, 0)
    for g in range(2):
        give(g).wait()


def focus(body, depth, taps, operands, weights, chirp, tables, rows, prior, name):
    inside, anywhere = pl.BlockSpec(memory_space=pltpu.VMEM), pl.BlockSpec(memory_space=pl.ANY)
    args = [taps, *operands, weights, chirp, *tables]
    specs = [pl.BlockSpec(memory_space=pltpu.SMEM)] + [inside] * (len(args) - 1)
    aliases = {}
    if prior is not None:
        aliases = {len(args): 0}
        specs.append(anywhere)
        args.append(prior)
    return pl.pallas_call(
        body,
        in_specs=specs,
        out_specs=anywhere,
        out_shape=jax.ShapeDtypeStruct((2, rows // 8, FACTOR, 8, FACTOR), jnp.float32),
        input_output_aliases=aliases,
        scratch_shapes=[
            pltpu.VMEM((depth, 2) + PADDED, jnp.float32),
            pltpu.VMEM((2, 2, FACTOR, 8, FACTOR), jnp.float32),
            pltpu.SemaphoreType.DMA((3,)),
        ],
        compiler_params=pltpu.CompilerParams(vmem_limit_bytes=26 << 20),
        cost_estimate=pl.CostEstimate(flops=6 << 30, bytes_accessed=8 << 20, transcendentals=0),
        name=name,
    )(*args)


def two_parts(values):
    high = lax.reduce_precision(values, 8, 7)
    return jnp.concatenate([high.astype(jnp.bfloat16), (values - high).astype(jnp.bfloat16)])


def turns(product, modulus):
    angle = 2.0 * math.pi / modulus * (product % modulus).astype(jnp.float32)
    return jnp.cos(angle), jnp.sin(angle)


def transform_tables(center, sign):
    start = (center - PULSES // 2) % PULSES
    index = jnp.arange(FACTOR, dtype=jnp.int32)
    fine, coarse = index + start % FACTOR, index + start // FACTOR

    def block(a, b):
        c, s = turns(a[:, None] * b[None, :], FACTOR)
        return two_parts(stack2(c, -sign * s, sign * s, c))

    if sign < 0:
        twist = turns(fine[:, None] * index[None, :], PULSES)
        return [block(fine, index), *twist, block(coarse, index)]
    twist = turns(index[:, None] * fine[None, :], PULSES)
    return [block(index, coarse), *twist, block(index, fine)]


def spectral_tables(distance, chirp_rate):
    index = jnp.arange(FACTOR, dtype=jnp.int32)
    bins = FACTOR * index[:, None] + index[None, :]
    relative = (bins - PULSES // 2).astype(jnp.float32) / PULSES
    migration = distance.astype(jnp.float32) * 4.0 * relative * relative
    nearness = jnp.array([(7 - edge(t)) ** 2 for t in range(TILES)], jnp.int32)
    latest = jnp.array([LASTS[t] - COUNTS[t] + 1 for t in range(TILES)], jnp.int32)
    taps = jnp.minimum(distance * nearness // (TILES * TILES // 4) - LOWER, latest)
    nearest = jnp.round(migration)
    sine = jnp.sin(math.pi * (migration - nearest)) / math.pi
    quarter = math.pi / TAPS
    offset = jnp.repeat(taps, 8)[None, :, None] + jnp.arange(max(COUNTS), dtype=jnp.int32)[:, None, None]
    away = offset.astype(jnp.float32) - migration
    sign = jnp.where((nearest.astype(jnp.int32) + offset) % 2 == 0, -1.0, 1.0)
    ratio = jnp.where(away == 0.0, 1.0, sign * sine / jnp.where(away == 0.0, 1.0, away))
    inside = jnp.abs(away) < TAPS
    weights = jnp.where(inside, ratio * (0.5 + 0.5 * jnp.cos(quarter * away)), 0.0)
    window = (0.54 + 0.46 * jnp.cos(2.0 * math.pi * relative)) / PULSES
    phase = math.pi * chirp_rate[:, None, None] * (relative * relative)
    weights = jnp.pad(weights, ((0, 0), (0, DEPTH - FACTOR), (0, 0)))
    return taps, weights, jnp.stack([window * jnp.cos(phase), window * jnp.sin(phase)], axis=1)


def compute(received, exchange, own, below, above, distance, chirp_rate):
    rows = received.shape[2]
    taps, weights, chirp = spectral_tables(distance, chirp_rate)
    inverse = transform_tables(own, 1)
    up, down = exchange(*halo(received, transform_tables(below, -1), transform_tables(above, -1)))
    spec = forward(received, transform_tables(own, -1))
    shared = (weights, chirp, inverse, rows)
    image = focus(inner_body, LOWER + 4 + UPPER, taps, [spec, down], *shared, None, "inner")
    image = focus(outer_body, LOWER + rows // 2 + UPPER, taps, [spec, up], *shared, image, "outer")
    return image.transpose(0, 1, 3, 2, 4).reshape(2, rows, PULSES)


def per_device(raw_echo, centroid, shifts, chirp_rate):
    devices = lax.axis_size("row")
    own_rows = raw_echo.shape[1] // devices
    blocks = raw_echo.reshape(2, devices, own_rows, raw_echo.shape[2])
    received = lax.all_to_all(arrange(blocks), "row", split_axis=0, concat_axis=0, tiled=True)

    def pick(values, device):
        block = jnp.clip(device, 0, devices - 1) * own_rows // BLOCK
        return jnp.sum(jnp.where(block == jnp.arange(values.shape[0], dtype=jnp.int32), values, 0))

    def exchange(up, down):
        return from_behind(up, "row", -1), from_behind(down, "row", 1)

    device = lax.axis_index("row")
    centers = [pick(centroid, device + by) for by in (0, -1, 1)]
    return compute(received, exchange, *centers, pick(shifts, device), chirp_rate)


def solution(mesh):
    return jax.shard_map(
        per_device,
        mesh=mesh,
        in_specs=(P(None, "slab", "row"), P("slab"), P("slab"), P(("slab", "row"))),
        out_specs=P(None, ("slab", "row"), None),
        check_vma=False,
    )
```

time: 163 us -> 162 us (level)
    pallas_call x4 -> x3, Pallas kernels: 19.2 us -> 17.4 us  [the longest x2 12.4 us: focus(): pl.pallas_call(body, in_specs=specs, out_specs=anywhere, out_shape=jax.Sh...]
    ppermute x2, waiting for transfers between devices: 0.01 us -> 1.73 us  [from_behind(): return lax.ppermute(shard, axis, pairs)]
  transfers between devices with their start and end apart: 3 -> 3, of which waited for: 1 -> 2; matrix products, arithmetic and copies ran while one was open for 12% -> 12% of each run, Pallas kernels for 10% -> 9%
where the time goes in v4:
time: 162 us
  waiting for transfers between devices  77 us (48%)
  starting transfers between devices  32.9 us (20%)
  Pallas kernels  28.7 us (18%)
  other arithmetic  19.4 us (12%)
  between operations  3.36 us (2%)
    all_to_all x1, waiting for transfers between devices, per_device(): lax.all_to_all(arrange(blocks), 'row', split_axis=0, concat_axis=0, tiled...  75.3 us
    all_to_all x1, starting transfers between devices, per_device(): lax.all_to_all(arrange(blocks), 'row', split_axis=0, concat_axis=0, tiled...  27.5 us
    pallas_call x2, Pallas kernels, focus(): pl.pallas_call(body, in_specs=specs, out_specs=anywhere, out_shape=jax.Sh...  12.4 us
    mul x1, other arithmetic, spectral_tables(): window * jnp.cos(phase)  7.68 us
    pallas_call x1, Pallas kernels, forward(): pl.pallas_call(forward_body, grid=(rows // 8,), in_specs=[pl.BlockSpec(me...  7.65 us
    ppermute x2, starting transfers between devices, from_behind(): return lax.ppermute(shard, axis, pairs)  5.44 us
    pallas_call x1, Pallas kernels, halo(): pl.pallas_call(halo_body, in_specs=[pl.BlockSpec(memory_space=pl.ANY)] +...  5.04 us
    pallas_call x1, Pallas kernels, arrange(): pl.pallas_call(arrange_body, in_specs=[pl.BlockSpec(memory_space=pl.ANY)]...  3.65 us
  transfers between devices with their start and end apart: 3, of which 2 were waited for; matrix products, arithmetic and copies ran while one was open for 12% of the time, Pallas kernels for 9%

profile of v4, /device:TPU:519, one launch (start us, length us, event | category | flops | bytes accessed | tf_op | source)
XLA Modules:
  0.0 161.6 jit_solution(1754644450442806407)
XLA Ops:
  0.0 3.7 %arrange.1 = f32[128,2,32,128]{3,2,1,0:T(8,128)} custom-call(f32[2,128,32,128]{3,2,1,0:T(8,128)} %bitcast.4), custom_call_target="tpu_custom_call" | custom-call | flops 1048576 | bytes 8388608 | tf_op jit(solution)/shard_map/arrange/pallas_call | solution.py:179
  3.7 0.0 copy-start.1
  3.7 0.0 copy-start.4
  3.7 0.0 copy-start.2
  3.7 0.0 copy-start.3
  3.7 27.5 %all-to-all-start = ((f32[128,2,32,128]{3,2,1,0:T(8,128)}), f32[128,2,32,128]{3,2,1,0:T(8,128)}, u32[]{:S(2)}, u32[]{:S(2)}) async-start(f32[128,2,32,128]{3,2,1,0:T(8,128)} %arrange.1), calls=%async_computation | async-start | bytes 8388608 | tf_op jit(solution)/shard_map/all_to_all | solution.py:412
  31.2 0.0 copy-done.1
  31.2 0.7 fusion.120
  33.9 0.0 copy-done.4
  33.9 0.7 fusion.117
  35.3 0.0 copy-done.2
  35.3 0.0 copy-done.3
  35.3 0.6 add_minimum_fusion.refs_0_
  36.0 0.1 broadcast_in_dim.23
  36.0 0.1 add.308
  36.2 0.5 add_multiply_fusion
  36.7 3.0 %fusion.4 = f32[11,128,128]{2,1,0:T(8,128)S(1)} fusion(f32[128,128]{1,0:T(8,128)S(1)} %get-tuple-element.48, s32[11,128]{1,0:T(8,128)S(1)} %get-tuple-element.52, s32[128,128]{1,0:T(8,128)S(1)} %get-tuple-element.47, f32[128,128]{1,0:T(8,128)S(1)} %get-tuple-element.50, f32[11,128]{1,0:T(8,128)S(1)} %get-tuple-element.51), kind=kLoop, calls=%fused_computation.16 | loop fusion | flops 4866048 | bytes 928768 | tf_op jit(solution)/shard_map/jit(_where)/select_n | solution.py:389
  39.7 0.1 pad.4.refs_3_
  39.9 0.6 broadcast_multiply_fusion.1
  40.4 0.1 reduce-precision_convert_fusion.1
  40.6 1.0 broadcast_multiply_fusion
  41.6 0.1 reduce-precision_convert_fusion
  41.8 0.3 fusion.104
  42.1 0.3 fusion.98
  42.5 0.0 copy-start.5
  42.5 0.6 fusion.106
  43.2 0.6 fusion.100
  43.9 0.0 copy-done.5
  43.9 7.7 %fusion = (f32[32,1,128,128]{3,2,1,0:T(8,128)S(1)}, f32[32,1,128,128]{3,2,1,0:T(8,128)S(1)}) fusion(f32[128,128]{1,0:T(8,128)S(1)} %get-tuple-element.49, f32[32]{0:T(128)S(1)} %broadcast_multiply_fusion.8, f32[128,128]{1,0:T(8,128)S(1)} %get-tuple-element.46), kind=kLoop, calls=%fused_computation.3 | loop fusion | flops 1572864 | bytes 4325504 | tf_op jit(solution)/shard_map/mul | solution.py:393
  51.6 2.2 %pad_maximum_fusion.refs_4_ = f32[32,2,128,128]{3,2,1,0:T(8,128)} fusion(f32[32,1,128,128]{3,2,1,0:T(8,128)S(1)} %get-tuple-element.29, f32[32,1,128,128]{3,2,1,0:T(8,128)S(1)} %get-tuple-element.28), kind=kLoop, calls=%fused_computation | loop fusion | flops 1048576 | bytes 8388608 | tf_op jit(solution)/shard_map/stack | solution.py:393
  53.8 75.3 %all-to-all-done.refs_0_ = f32[128,2,32,128]{3,2,1,0:T(8,128)} async-done(((f32[128,2,32,128]{3,2,1,0:T(8,128)}), f32[128,2,32,128]{3,2,1,0:T(8,128)}, u32[]{:S(2)}, u32[]{:S(2)}) %all-to-all-start) | async-done | bytes 4194336 | tf_op jit(solution)/shard_map/all_to_all | solution.py:412
  129.1 5.0 %halo.1 = (f32[2,1040,128]{2,1,0:T(8,128)S(1)}, f32[3,2,128,128]{3,2,1,0:T(8,128)S(1)}) custom-call(f32[128,2,32,128]{3,2,1,0:T(8,128)} %all-to-all-done.refs_0_, bf16[512,256]{1,0:T(8,128)(2,1)S(1)} %get-tuple-element.73.refs_1_, f32[128,128]{1,0:T(8,128)S(1)} %get-tuple-element.68.refs_2_, f32[128,128]{1,0:T(8,128)S(1)} %get-tuple-element.64.refs_3_, ...), custom_call_target="tpu_custom_call" | custom-call | flops 5368709120 | bytes 5242880 | tf_op jit(solution)/shard_map/halo/pallas_call | solution.py:143
  134.2 3.5 %collective-permute-start.1 = (f32[3,2,128,128]{3,2,1,0:T(8,128)S(1)}, f32[3,2,128,128]{3,2,1,0:T(8,128)S(1)}, u32[]{:S(2)}, u32[]{:S(2)}) collective-permute-start(f32[3,2,128,128]{3,2,1,0:T(8,128)S(1)} %get-tuple-element.8), channel_id=1, source_target_pairs={{0,1},{1,2},{2,3},{3,4},{4,5},{5,6},{6,7},{7,8},{8,9},{9,10},{10,1... | collective-permute-start | bytes 1179656 | tf_op jit(solution)/shard_map/ppermute | solution.py:51
  137.7 2.0 %collective-permute-start = (f32[2,1040,128]{2,1,0:T(8,128)S(1)}, f32[2,1040,128]{2,1,0:T(8,128)S(1)}, u32[]{:S(2)}, u32[]{:S(2)}) collective-permute-start(f32[2,1040,128]{2,1,0:T(8,128)S(1)} %get-tuple-element.7), channel_id=1, source_target_pairs={{1,0},{2,1},{3,2},{4,3},{5,4},{6,5},{7,6},{8,7},{9,8},{10,9},{11,1... | collective-permute-start | bytes 3194888 | tf_op jit(solution)/shard_map/ppermute | solution.py:51
  139.6 0.0 copy-start
  139.6 7.7 %forward.1.refs_1_ = f32[32,2,136,128]{3,2,1,0:T(8,128)S(1)} custom-call(f32[128,2,32,128]{3,2,1,0:T(8,128)} %all-to-all-done.refs_0_, bf16[512,256]{1,0:T(8,128)(2,1)S(1)} %pad_maximum_fusion.1.refs_1_, f32[128,128]{1,0:T(8,128)S(1)} %get-tuple-element.39.refs_2_, f32[128,128]{1,0:T(8,128)S(1)} %get-tuple-element.33.refs_3_, ...), custom_call_target="tpu_custom_call" | custom-call | flops 8589934592 | bytes 8388608 | tf_op jit(solution)/shard_map/forward/pallas_call | solution.py:221
  147.3 0.0 collective-permute-done.1.refs_2_
  147.3 0.0 copy-done
  147.3 6.1 %inner.1.refs_9_ = f32[2,4,128,8,128]{4,3,2,1,0:T(8,128)} custom-call(s32[16]{0:T(128)S(1)} %add_minimum_fusion.refs_0_, f32[32,2,136,128]{3,2,1,0:T(8,128)S(1)} %forward.1.refs_1_, f32[3,2,128,128]{3,2,1,0:T(8,128)S(1)} %collective-permute-done.1.refs_2_, f32[11,136,128]{2,1,0:T(8,128)S(1)} %pad.4.refs_3_, f32[32,2,128,128]{3,2,1,0:T(8,128)S(1)} %copy-done, ...), custom_call_target="tpu_custom_call" | custom-call | flops 6442450944 | bytes 8388608 | tf_op jit(solution)/shard_map/inner/pallas_call | solution.py:330
  153.5 1.7 %collective-permute-done.refs_2_ = f32[2,1040,128]{2,1,0:T(8,128)S(1)} collective-permute-done((f32[2,1040,128]{2,1,0:T(8,128)S(1)}, f32[2,1040,128]{2,1,0:T(8,128)S(1)}, u32[]{:S(2)}, u32[]{:S(2)}) %collective-permute-start) | collective-permute-done | bytes 1064992 | tf_op jit(solution)/shard_map/ppermute | solution.py:51
  155.2 6.2 %outer.1 = f32[2,4,128,8,128]{4,3,2,1,0:T(8,128)} custom-call(s32[16]{0:T(128)S(1)} %add_minimum_fusion.refs_0_, f32[32,2,136,128]{3,2,1,0:T(8,128)S(1)} %forward.1.refs_1_, f32[2,1040,128]{2,1,0:T(8,128)S(1)} %collective-permute-done.refs_2_, f32[11,136,128]{2,1,0:T(8,128)S(1)} %pad.4.refs_3_, ...), custom_call_target="tpu_custom_call", output_to_operand_aliasing={{}: (9, {})} | custom-call | flops 6442450944 | bytes 8388608 | tf_op jit(solution)/shard_map/outer/pallas_call | solution.py:330
  (19 shorter events, 0.3 us)
Async XLA Ops:
  3.7 27.6 %copy-start.1 = (s32[32]{0:T(128)S(1)}, s32[32]{0:T(128)}, u32[]{:S(2)}) copy-start(s32[32]{0:T(128)} %param.7) | copy-start | bytes 388
  3.7 30.3 %copy-start.4 = (s32[32]{0:T(128)S(1)}, s32[32]{0:T(128)}, u32[]{:S(2)}) copy-start(s32[32]{0:T(128)} %param.8) | copy-start | bytes 388
  3.7 31.6 %copy-start.2 = (s32[16]{0:T(128)S(1)}, s32[16]{0:T(128)}, u32[]{:S(2)}) copy-start(s32[16]{0:T(128)} %constant.248.clone) | copy-start | bytes 196
  3.7 31.6 %copy-start.3 = (s32[16]{0:T(128)S(1)}, s32[16]{0:T(128)}, u32[]{:S(2)}) copy-start(s32[16]{0:T(128)} %constant.247.clone) | copy-start | bytes 196
  3.7 125.4 %all-to-all-start = ((f32[128,2,32,128]{3,2,1,0:T(8,128)}), f32[128,2,32,128]{3,2,1,0:T(8,128)}, u32[]{:S(2)}, u32[]{:S(2)}) async-start(f32[128,2,32,128]{3,2,1,0:T(8,128)} %arrange.1), calls=%async_computation | async-start | bytes 8388608 | tf_op jit(solution)/shard_map/all_to_all | solution.py:412
  42.5 1.4 copy-start.5
  134.2 13.1 %collective-permute-start.1 = (f32[3,2,128,128]{3,2,1,0:T(8,128)S(1)}, f32[3,2,128,128]{3,2,1,0:T(8,128)S(1)}, u32[]{:S(2)}, u32[]{:S(2)}) collective-permute-start(f32[3,2,128,128]{3,2,1,0:T(8,128)S(1)} %get-tuple-element.8), channel_id=1, source_target_pairs={{0,1},{1,2},{2,3},{3,4},{4,5},{5,6},{6,7},{7,8},{8,9},{9,10},{10,1... | collective-permute-start | bytes 1179656 | tf_op jit(solution)/shard_map/ppermute | solution.py:51
  137.7 17.5 %collective-permute-start = (f32[2,1040,128]{2,1,0:T(8,128)S(1)}, f32[2,1040,128]{2,1,0:T(8,128)S(1)}, u32[]{:S(2)}, u32[]{:S(2)}) collective-permute-start(f32[2,1040,128]{2,1,0:T(8,128)S(1)} %get-tuple-element.7), channel_id=1, source_target_pairs={{1,0},{2,1},{3,2},{4,3},{5,4},{6,5},{7,6},{8,7},{9,8},{10,9},{11,1... | collective-permute-start | bytes 3194888 | tf_op jit(solution)/shard_map/ppermute | solution.py:51
  139.6 7.7 %copy-start = (f32[32,2,128,128]{3,2,1,0:T(8,128)S(1)}, f32[32,2,128,128]{3,2,1,0:T(8,128)}, u32[]{:S(2)}) copy-start(f32[32,2,128,128]{3,2,1,0:T(8,128)} %pad_maximum_fusion.refs_4_) | copy-start | bytes 12582916

commit v5 on v4

--- a/solution.py
+++ b/solution.py
@@ -19,7 +19,6 @@
 PLANE = (FACTOR, FACTOR)
 DEPTH = FACTOR + 8
 PADDED = (DEPTH, FACTOR)
-TABLE = (2 * FACTOR, 2 * FACTOR)
 
 
 def edge(tile):
@@ -318,7 +317,7 @@
         give(g).wait()
 
 
-def focus(body, depth, taps, operands, weights, chirp, tables, rows, prior, name):
+def focus(body, depth, taps, operands, weights, chirp, tables, rows, prior):
     inside, anywhere = pl.BlockSpec(memory_space=pltpu.VMEM), pl.BlockSpec(memory_space=pl.ANY)
     args = [taps, *operands, weights, chirp, *tables]
     specs = [pl.BlockSpec(memory_space=pltpu.SMEM)] + [inside] * (len(args) - 1)
@@ -340,7 +339,6 @@
         ],
         compiler_params=pltpu.CompilerParams(vmem_limit_bytes=26 << 20),
         cost_estimate=pl.CostEstimate(flops=6 << 30, bytes_accessed=8 << 20, transcendentals=0),
-        name=name,
     )(*args)
 
 
@@ -400,8 +398,8 @@
     up, down = exchange(*halo(received, transform_tables(below, -1), transform_tables(above, -1)))
     spec = forward(received, transform_tables(own, -1))
     shared = (weights, chirp, inverse, rows)
-    image = focus(inner_body, LOWER + 4 + UPPER, taps, [spec, down], *shared, None, "inner")
-    image = focus(outer_body, LOWER + rows // 2 + UPPER, taps, [spec, up], *shared, image, "outer")
+    image = focus(inner_body, LOWER + 4 + UPPER, taps, [spec, down], *shared, None)
+    image = focus(outer_body, LOWER + rows // 2 + UPPER, taps, [spec, up], *shared, image)
     return image.transpose(0, 1, 3, 2, 4).reshape(2, rows, PULSES)
 
 
@@ -416,7 +414,9 @@
         return jnp.sum(jnp.where(block == jnp.arange(values.shape[0], dtype=jnp.int32), values, 0))
 
     def exchange(up, down):
-        return from_behind(up, "row", -1), from_behind(down, "row", 1)
+        up = from_behind(up, "row", -1)
+        down = from_behind(down, "row", 1)
+        return up, down
 
     device = lax.axis_index("row")
     centers = [pick(centroid, device + by) for by in (0, -1, 1)]

time: 162 us -> 162 us (level)
  no operation moved by 1% of the time
where the time goes in v5:
time: 162 us
  waiting for transfers between devices  77 us (48%)
  starting transfers between devices  32.9 us (20%)
  Pallas kernels  28.8 us (18%)
  other arithmetic  19.4 us (12%)
  between operations  3.36 us (2%)
    all_to_all x1, waiting for transfers between devices, per_device(): lax.all_to_all(arrange(blocks), 'row', split_axis=0, concat_axis=0, tiled...  75.3 us
    all_to_all x1, starting transfers between devices, per_device(): lax.all_to_all(arrange(blocks), 'row', split_axis=0, concat_axis=0, tiled...  27.5 us
    pallas_call x2, Pallas kernels, focus(): pl.pallas_call(body, in_specs=specs, out_specs=anywhere, out_shape=jax.Sh...  12.4 us
    mul x1, other arithmetic, spectral_tables(): window * jnp.cos(phase)  7.68 us
    pallas_call x1, Pallas kernels, forward(): pl.pallas_call(forward_body, grid=(rows // 8,), in_specs=[pl.BlockSpec(me...  7.65 us
    ppermute x2, starting transfers between devices, from_behind(): return lax.ppermute(shard, axis, pairs)  5.44 us
    pallas_call x1, Pallas kernels, halo(): pl.pallas_call(halo_body, in_specs=[pl.BlockSpec(memory_space=pl.ANY)] +...  5.04 us
    pallas_call x1, Pallas kernels, arrange(): pl.pallas_call(arrange_body, in_specs=[pl.BlockSpec(memory_space=pl.ANY)]...  3.65 us
  transfers between devices with their start and end apart: 3, of which 2 were waited for; matrix products, arithmetic and copies ran while one was open for 12% of the time, Pallas kernels for 9%

profile of v5, /device:TPU:519, one launch (start us, length us, event | category | flops | bytes accessed | tf_op | source)
XLA Modules:
  0.0 161.7 jit_solution(1754644450442806407)
XLA Ops:
  0.0 3.7 %arrange.1 = f32[128,2,32,128]{3,2,1,0:T(8,128)} custom-call(f32[2,128,32,128]{3,2,1,0:T(8,128)} %bitcast.4), custom_call_target="tpu_custom_call" | custom-call | flops 1048576 | bytes 8388608 | tf_op jit(solution)/shard_map/arrange/pallas_call | solution.py:178
  3.7 0.0 copy-start.1
  3.7 0.0 copy-start.4
  3.7 0.0 copy-start.2
  3.7 0.0 copy-start.3
  3.7 27.5 %all-to-all-start = ((f32[128,2,32,128]{3,2,1,0:T(8,128)}), f32[128,2,32,128]{3,2,1,0:T(8,128)}, u32[]{:S(2)}, u32[]{:S(2)}) async-start(f32[128,2,32,128]{3,2,1,0:T(8,128)} %arrange.1), calls=%async_computation | async-start | bytes 8388608 | tf_op jit(solution)/shard_map/all_to_all | solution.py:410
  31.2 0.0 copy-done.1
  31.2 0.7 fusion.120
  33.9 0.0 copy-done.4
  33.9 0.7 fusion.117
  35.3 0.0 copy-done.2
  35.3 0.0 copy-done.3
  35.3 0.6 add_minimum_fusion.refs_0_
  36.0 0.1 broadcast_in_dim.23
  36.0 0.1 add.308
  36.2 0.5 add_multiply_fusion
  36.7 3.0 %fusion.4 = f32[11,128,128]{2,1,0:T(8,128)S(1)} fusion(f32[128,128]{1,0:T(8,128)S(1)} %get-tuple-element.48, s32[11,128]{1,0:T(8,128)S(1)} %get-tuple-element.52, s32[128,128]{1,0:T(8,128)S(1)} %get-tuple-element.47, f32[128,128]{1,0:T(8,128)S(1)} %get-tuple-element.50, f32[11,128]{1,0:T(8,128)S(1)} %get-tuple-element.51), kind=kLoop, calls=%fused_computation.16 | loop fusion | flops 4866048 | bytes 928768 | tf_op jit(solution)/shard_map/jit(_where)/select_n | solution.py:387
  39.7 0.1 pad.4.refs_3_
  39.9 0.6 broadcast_multiply_fusion.1
  40.4 0.1 reduce-precision_convert_fusion.1
  40.6 1.0 broadcast_multiply_fusion
  41.6 0.1 reduce-precision_convert_fusion
  41.8 0.3 fusion.104
  42.1 0.3 fusion.98
  42.5 0.0 copy-start.5
  42.5 0.6 fusion.106
  43.2 0.6 fusion.100
  43.9 0.0 copy-done.5
  43.9 7.7 %fusion = (f32[32,1,128,128]{3,2,1,0:T(8,128)S(1)}, f32[32,1,128,128]{3,2,1,0:T(8,128)S(1)}) fusion(f32[128,128]{1,0:T(8,128)S(1)} %get-tuple-element.49, f32[32]{0:T(128)S(1)} %broadcast_multiply_fusion.8, f32[128,128]{1,0:T(8,128)S(1)} %get-tuple-element.46), kind=kLoop, calls=%fused_computation.3 | loop fusion | flops 1572864 | bytes 4325504 | tf_op jit(solution)/shard_map/mul | solution.py:391
  51.6 2.2 %pad_maximum_fusion.refs_4_ = f32[32,2,128,128]{3,2,1,0:T(8,128)} fusion(f32[32,1,128,128]{3,2,1,0:T(8,128)S(1)} %get-tuple-element.29, f32[32,1,128,128]{3,2,1,0:T(8,128)S(1)} %get-tuple-element.28), kind=kLoop, calls=%fused_computation | loop fusion | flops 1048576 | bytes 8388608 | tf_op jit(solution)/shard_map/stack | solution.py:391
  53.8 75.3 %all-to-all-done.refs_0_ = f32[128,2,32,128]{3,2,1,0:T(8,128)} async-done(((f32[128,2,32,128]{3,2,1,0:T(8,128)}), f32[128,2,32,128]{3,2,1,0:T(8,128)}, u32[]{:S(2)}, u32[]{:S(2)}) %all-to-all-start) | async-done | bytes 4194336 | tf_op jit(solution)/shard_map/all_to_all | solution.py:410
  129.1 5.0 %halo.1 = (f32[2,1040,128]{2,1,0:T(8,128)S(1)}, f32[3,2,128,128]{3,2,1,0:T(8,128)S(1)}) custom-call(f32[128,2,32,128]{3,2,1,0:T(8,128)} %all-to-all-done.refs_0_, bf16[512,256]{1,0:T(8,128)(2,1)S(1)} %get-tuple-element.73.refs_1_, f32[128,128]{1,0:T(8,128)S(1)} %get-tuple-element.68.refs_2_, f32[128,128]{1,0:T(8,128)S(1)} %get-tuple-element.64.refs_3_, ...), custom_call_target="tpu_custom_call" | custom-call | flops 5368709120 | bytes 5242880 | tf_op jit(solution)/shard_map/halo/pallas_call | solution.py:142
  134.2 3.5 %collective-permute-start.1 = (f32[3,2,128,128]{3,2,1,0:T(8,128)S(1)}, f32[3,2,128,128]{3,2,1,0:T(8,128)S(1)}, u32[]{:S(2)}, u32[]{:S(2)}) collective-permute-start(f32[3,2,128,128]{3,2,1,0:T(8,128)S(1)} %get-tuple-element.8), channel_id=1, source_target_pairs={{0,1},{1,2},{2,3},{3,4},{4,5},{5,6},{6,7},{7,8},{8,9},{9,10},{10,1... | collective-permute-start | bytes 1179656 | tf_op jit(solution)/shard_map/ppermute | solution.py:50
  137.7 2.0 %collective-permute-start = (f32[2,1040,128]{2,1,0:T(8,128)S(1)}, f32[2,1040,128]{2,1,0:T(8,128)S(1)}, u32[]{:S(2)}, u32[]{:S(2)}) collective-permute-start(f32[2,1040,128]{2,1,0:T(8,128)S(1)} %get-tuple-element.7), channel_id=1, source_target_pairs={{1,0},{2,1},{3,2},{4,3},{5,4},{6,5},{7,6},{8,7},{9,8},{10,9},{11,1... | collective-permute-start | bytes 3194888 | tf_op jit(solution)/shard_map/ppermute | solution.py:50
  139.6 0.0 copy-start
  139.6 7.7 %forward.1.refs_1_ = f32[32,2,136,128]{3,2,1,0:T(8,128)S(1)} custom-call(f32[128,2,32,128]{3,2,1,0:T(8,128)} %all-to-all-done.refs_0_, bf16[512,256]{1,0:T(8,128)(2,1)S(1)} %pad_maximum_fusion.1.refs_1_, f32[128,128]{1,0:T(8,128)S(1)} %get-tuple-element.39.refs_2_, f32[128,128]{1,0:T(8,128)S(1)} %get-tuple-element.33.refs_3_, ...), custom_call_target="tpu_custom_call" | custom-call | flops 8589934592 | bytes 8388608 | tf_op jit(solution)/shard_map/forward/pallas_call | solution.py:220
  147.3 0.0 collective-permute-done.1.refs_2_
  147.3 0.0 copy-done
  147.3 6.2 %shard_map.64.refs_9_ = f32[2,4,128,8,128]{4,3,2,1,0:T(8,128)} custom-call(s32[16]{0:T(128)S(1)} %add_minimum_fusion.refs_0_, f32[32,2,136,128]{3,2,1,0:T(8,128)S(1)} %forward.1.refs_1_, f32[3,2,128,128]{3,2,1,0:T(8,128)S(1)} %collective-permute-done.1.refs_2_, f32[11,136,128]{2,1,0:T(8,128)S(1)} %pad.4.refs_3_, f32[32,2,128,128]{3,2,1,0:T(8,128)S(1)} %copy-done, ...), custom_call_target="tpu_custom_call" | custom-call | flops 6442450944 | bytes 8388608 | tf_op jit(solution)/shard_map/pallas_call | solution.py:329
  153.5 1.7 %collective-permute-done.refs_2_ = f32[2,1040,128]{2,1,0:T(8,128)S(1)} collective-permute-done((f32[2,1040,128]{2,1,0:T(8,128)S(1)}, f32[2,1040,128]{2,1,0:T(8,128)S(1)}, u32[]{:S(2)}, u32[]{:S(2)}) %collective-permute-start) | collective-permute-done | bytes 1064992 | tf_op jit(solution)/shard_map/ppermute | solution.py:50
  155.2 6.2 %shard_map.65 = f32[2,4,128,8,128]{4,3,2,1,0:T(8,128)} custom-call(s32[16]{0:T(128)S(1)} %add_minimum_fusion.refs_0_, f32[32,2,136,128]{3,2,1,0:T(8,128)S(1)} %forward.1.refs_1_, f32[2,1040,128]{2,1,0:T(8,128)S(1)} %collective-permute-done.refs_2_, f32[11,136,128]{2,1,0:T(8,128)S(1)} %pad.4.refs_3_, ...), custom_call_target="tpu_custom_call", output_to_operand_aliasing={{}: (9, {})} | custom-call | flops 6442450944 | bytes 8388608 | tf_op jit(solution)/shard_map/pallas_call | solution.py:329
  (19 shorter events, 0.3 us)
Async XLA Ops:
  3.7 27.6 %copy-start.1 = (s32[32]{0:T(128)S(1)}, s32[32]{0:T(128)}, u32[]{:S(2)}) copy-start(s32[32]{0:T(128)} %param.7) | copy-start | bytes 388
  3.7 30.3 %copy-start.4 = (s32[32]{0:T(128)S(1)}, s32[32]{0:T(128)}, u32[]{:S(2)}) copy-start(s32[32]{0:T(128)} %param.8) | copy-start | bytes 388
  3.7 31.6 %copy-start.2 = (s32[16]{0:T(128)S(1)}, s32[16]{0:T(128)}, u32[]{:S(2)}) copy-start(s32[16]{0:T(128)} %constant.248.clone) | copy-start | bytes 196
  3.7 31.6 %copy-start.3 = (s32[16]{0:T(128)S(1)}, s32[16]{0:T(128)}, u32[]{:S(2)}) copy-start(s32[16]{0:T(128)} %constant.247.clone) | copy-start | bytes 196
  3.7 125.4 %all-to-all-start = ((f32[128,2,32,128]{3,2,1,0:T(8,128)}), f32[128,2,32,128]{3,2,1,0:T(8,128)}, u32[]{:S(2)}, u32[]{:S(2)}) async-start(f32[128,2,32,128]{3,2,1,0:T(8,128)} %arrange.1), calls=%async_computation | async-start | bytes 8388608 | tf_op jit(solution)/shard_map/all_to_all | solution.py:410
  42.5 1.4 copy-start.5
  134.2 13.1 %collective-permute-start.1 = (f32[3,2,128,128]{3,2,1,0:T(8,128)S(1)}, f32[3,2,128,128]{3,2,1,0:T(8,128)S(1)}, u32[]{:S(2)}, u32[]{:S(2)}) collective-permute-start(f32[3,2,128,128]{3,2,1,0:T(8,128)S(1)} %get-tuple-element.8), channel_id=1, source_target_pairs={{0,1},{1,2},{2,3},{3,4},{4,5},{5,6},{6,7},{7,8},{8,9},{9,10},{10,1... | collective-permute-start | bytes 1179656 | tf_op jit(solution)/shard_map/ppermute | solution.py:50
  137.7 17.5 %collective-permute-start = (f32[2,1040,128]{2,1,0:T(8,128)S(1)}, f32[2,1040,128]{2,1,0:T(8,128)S(1)}, u32[]{:S(2)}, u32[]{:S(2)}) collective-permute-start(f32[2,1040,128]{2,1,0:T(8,128)S(1)} %get-tuple-element.7), channel_id=1, source_target_pairs={{1,0},{2,1},{3,2},{4,3},{5,4},{6,5},{7,6},{8,7},{9,8},{10,9},{11,1... | collective-permute-start | bytes 3194888 | tf_op jit(solution)/shard_map/ppermute | solution.py:50
  139.6 7.7 %copy-start = (f32[32,2,128,128]{3,2,1,0:T(8,128)S(1)}, f32[32,2,128,128]{3,2,1,0:T(8,128)}, u32[]{:S(2)}) copy-start(f32[32,2,128,128]{3,2,1,0:T(8,128)} %pad_maximum_fusion.refs_4_) | copy-start | bytes 12582916
